TPU v7x, 768 devices: a whole 4x8x12 slice. The times are simulated.
768 devices in a mesh: gx: 4 (over x), gy: 12 (over z_lo, core), gz: 16 (over z_hi, y).
Axes of the slice: x: 4, y: 8, z: 12 (z_hi: 2, z_lo: 6; z = z_hi * 6 + z_lo), core: 2. Of those that a mesh axis runs over, the one named last changes fastest.
Arguments:
- conserved: float32 [5, 64, 96, 512], P(None, 'gz', 'gy', 'gx'), may hold values from -3 to 12, as said below
- metrics: float32 [9, 64, 96, 512], P(None, 'gz', 'gy', 'gx'), may hold values from -0.6 to 2, as said below
- inv_volume: float32 [64, 96, 512], P('gz', 'gy', 'gx'), may hold values from 0.5 to 2
- wake_donor: int32 [512], P('gx'), may hold values from -1 to 511, as said below
Outputs:
- section_state: float32 [5, 64, 96, 512], P(None, 'gz', 'gy', 'gx')
- time_rate: float32 [5, 64, 96, 512], P(None, 'gz', 'gy', 'gx')
Inputs may be any that keep to these rules, and one draw needn't show every extreme that they name: `conserved`: each cell holds density rho of 0.5 to 2, pressure p of 0.5 to 2 and velocity components u of -1.5 to 1.5 as (rho, rho u, p / 0.4 + rho |u|^2 / 2). `metrics`: in each cell, row d (entries 3 d to 3 d + 2) has its entry 3 d + d between 0.5 and 2 and its other two entries at most 0.3 times that entry in magnitude. wake_donor[i] is either 512 - 1 - i or -1, and wake_donor[i] >= 0 exactly where wake_donor[511 - i] >= 0.
All inputs are finite; a program needn't handle non-finite values.
Results may differ from a plain program's by a relative error of at most 0.0001.
Values sent between devices are 32-bit elements; how exact they have to be, the bound alone decides.
A program may use at most 32 MiB of HBM per device.

v0:
```python
import jax
import jax.numpy as jnp
from jax import lax
from jax.sharding import PartitionSpec as P

GAMMA = 1.4
WENO_EPS = 1e-06
STEP_SIZE = 0.08


def from_partner(x, axis, bit):
    return lax.ppermute(x, axis, [(i, i ^ 1 << bit) for i in range(lax.axis_size(axis))])


def padded(block, sides, width, periodic):
    for axis, dim in sides:
        count = lax.axis_size(axis)
        forward = [(i, i + 1) for i in range(count - 1)]
        if periodic:
            forward.append((count - 1, 0))
        backward = [(target, source) for source, target in forward]
        low = lax.ppermute(
            lax.slice_in_dim(block, block.shape[dim] - width, None, axis=dim), axis, forward
        )
        high = lax.ppermute(lax.slice_in_dim(block, 0, width, axis=dim), axis, backward)
        block = jnp.concatenate([low, block, high], axis=dim)
    return block


def slab_of(values, start, amount, axis):
    return lax.slice_in_dim(values, start, start + amount, axis=values.ndim + axis)


def cross_of(first, second):
    return [
        first[1] * second[2] - first[2] * second[1],
        first[2] * second[0] - first[0] * second[2],
        first[0] * second[1] - first[1] * second[0],
    ]


def inner_of(first, second):
    return first[0] * second[0] + first[1] * second[1] + first[2] * second[2]


def cell_terms(fields, metric_row):
    density = fields[0]
    velocity = fields[1:4] / density
    kinetic = 0.5 * jnp.sum(fields[1:4] * velocity, axis=0)
    pressure = (GAMMA - 1.0) * (fields[4] - kinetic)
    contra = jnp.sum(metric_row * velocity, axis=0)
    fluxes = jnp.stack(
        [
            fields[0] * contra,
            fields[1] * contra + metric_row[0] * pressure,
            fields[2] * contra + metric_row[1] * pressure,
            fields[3] * contra + metric_row[2] * pressure,
            (fields[4] + pressure) * contra,
        ]
    )
    sound_speed = jnp.sqrt(GAMMA * pressure / density)
    speeds = jnp.abs(contra) + sound_speed * jnp.sqrt(jnp.sum(metric_row * metric_row, axis=0))
    primitive = jnp.concatenate([density[None], velocity, pressure[None]], axis=0)
    return (primitive, fluxes, speeds)


def eigen_pair(state, metric_row, pick):
    density = state[0]
    velocity = [state[1], state[2], state[3]]
    pressure = state[4]
    row_size = jnp.sqrt(metric_row[0] ** 2 + metric_row[1] ** 2 + metric_row[2] ** 2)
    normal = [metric_row[member] / row_size for member in range(3)]
    axis_unit = [1.0 if member == pick else 0.0 for member in range(3)]
    raw_cross = cross_of(normal, axis_unit)
    raw_size = jnp.sqrt(raw_cross[0] ** 2 + raw_cross[1] ** 2 + raw_cross[2] ** 2)
    tangent = [raw_cross[member] / raw_size for member in range(3)]
    binormal = cross_of(normal, tangent)
    sound_speed = jnp.sqrt(GAMMA * pressure / density)
    inverse = 1.0 / sound_speed
    kinetic = 0.5 * inner_of(velocity, velocity)
    enthalpy = GAMMA / (GAMMA - 1.0) * pressure / density + kinetic
    normal_speed = inner_of(normal, velocity)
    tangent_speed = inner_of(tangent, velocity)
    binormal_speed = inner_of(binormal, velocity)
    factor = (GAMMA - 1.0) * inverse * inverse
    scaled = factor * kinetic
    left_rows = [
        [0.5 * (scaled + normal_speed * inverse)]
        + [0.5 * (-factor * velocity[member] - normal[member] * inverse) for member in range(3)]
        + [0.5 * factor],
        [1.0 - scaled] + [factor * velocity[member] for member in range(3)] + [-factor],
        [-tangent_speed] + tangent + [0.0],
        [-binormal_speed] + binormal + [0.0],
        [0.5 * (scaled - normal_speed * inverse)]
        + [0.5 * (-factor * velocity[member] + normal[member] * inverse) for member in range(3)]
        + [0.5 * factor],
    ]
    right_columns = [
        [1.0]
        + [velocity[member] - sound_speed * normal[member] for member in range(3)]
        + [enthalpy - sound_speed * normal_speed],
        [1.0] + velocity + [kinetic],
        [0.0] + tangent + [tangent_speed],
        [0.0] + binormal + [binormal_speed],
        [1.0]
        + [velocity[member] + sound_speed * normal[member] for member in range(3)]
        + [enthalpy + sound_speed * normal_speed],
    ]
    return (left_rows, right_columns)


def project_left(matrix, vector):
    return jnp.stack(
        [
            sum((matrix[member][second] * vector[second] for second in range(5)))
            for member in range(5)
        ]
    )


def apply_right(matrix, vector):
    return jnp.stack(
        [
            sum((matrix[second][member] * vector[second] for second in range(5)))
            for member in range(5)
        ]
    )


def weno_side(stencil):
    far_left, near_left, center, near_right, far_right = stencil
    guess_zero = (2.0 * far_left - 7.0 * near_left + 11.0 * center) / 6.0
    guess_one = (-near_left + 5.0 * center + 2.0 * near_right) / 6.0
    guess_two = (2.0 * center + 5.0 * near_right - far_right) / 6.0
    smooth_zero = (
        13.0 / 12.0 * (far_left - 2.0 * near_left + center) ** 2
        + 0.25 * (far_left - 4.0 * near_left + 3.0 * center) ** 2
    )
    smooth_one = (
        13.0 / 12.0 * (near_left - 2.0 * center + near_right) ** 2
        + 0.25 * (near_left - near_right) ** 2
    )
    smooth_two = (
        13.0 / 12.0 * (center - 2.0 * near_right + far_right) ** 2
        + 0.25 * (3.0 * center - 4.0 * near_right + far_right) ** 2
    )
    weight_zero = 0.1 / (WENO_EPS + smooth_zero) ** 2
    weight_one = 0.6 / (WENO_EPS + smooth_one) ** 2
    weight_two = 0.3 / (WENO_EPS + smooth_two) ** 2
    return (weight_zero * guess_zero + weight_one * guess_one + weight_two * guess_two) / (
        weight_zero + weight_one + weight_two
    )


def interface_flux(fields, metric_row, axis, pick):
    primitive, fluxes, speeds = cell_terms(fields, metric_row)
    faces_count = fields.shape[fields.ndim + axis] - 5
    mean_state = 0.5 * (
        slab_of(primitive, 2, faces_count, axis) + slab_of(primitive, 3, faces_count, axis)
    )
    mean_row = 0.5 * (
        slab_of(metric_row, 2, faces_count, axis) + slab_of(metric_row, 3, faces_count, axis)
    )
    left_rows, right_columns = eigen_pair(mean_state, mean_row, pick)
    max_speed = slab_of(speeds, 0, faces_count, axis)
    for offset in range(1, 6):
        max_speed = jnp.maximum(max_speed, slab_of(speeds, offset, faces_count, axis))
    upwind = []
    downwind = []
    for offset in range(6):
        state_chars = project_left(left_rows, slab_of(fields, offset, faces_count, axis))
        flux_chars = project_left(left_rows, slab_of(fluxes, offset, faces_count, axis))
        upwind.append(0.5 * (flux_chars + max_speed * state_chars))
        downwind.append(0.5 * (flux_chars - max_speed * state_chars))
    combined = weno_side(upwind[0:5]) + weno_side(downwind[5:0:-1])
    return apply_right(right_columns, combined)


def divergence(fields, metric_row, axis, pick):
    face_flux = interface_flux(fields, metric_row, axis, pick)
    cells_count = face_flux.shape[face_flux.ndim + axis] - 1
    return slab_of(face_flux, 1, cells_count, axis) - slab_of(face_flux, 0, cells_count, axis)


def fix_ends(extended, at_start, at_end):
    interior = extended[..., 3:-3]
    lower_ghost = jnp.where(at_start, jnp.repeat(interior[..., :1], 3, axis=-1), extended[..., :3])
    upper_ghost = jnp.where(at_end, jnp.repeat(interior[..., -1:], 3, axis=-1), extended[..., -3:])
    return jnp.concatenate([lower_ghost, interior, upper_ghost], axis=-1)


def fix_wall(extended, ghosts, at_start, at_end):
    interior = extended[:, :, 3:-3, :]
    lower_ghost = jnp.where(at_start, ghosts, extended[:, :, :3, :])
    upper_ghost = jnp.where(
        at_end, jnp.repeat(interior[:, :, -1:, :], 3, axis=2), extended[:, :, -3:, :]
    )
    return jnp.concatenate([lower_ghost, interior, upper_ghost], axis=2)


def local(conserved, metrics, inv_volume, wake_donor):
    at_inflow = lax.axis_index("gx") == 0
    at_outflow = lax.axis_index("gx") == lax.axis_size("gx") - 1
    at_wall = lax.axis_index("gy") == 0
    at_top = lax.axis_index("gy") == lax.axis_size("gy") - 1
    mirrored = jnp.concatenate([conserved[:, :, 2::-1, :], metrics[3:6, :, 2::-1, :]], axis=0)
    for bit_number in range(lax.axis_size("gx").bit_length() - 1):
        mirrored = from_partner(mirrored, "gx", bit_number)
    mirrored = mirrored[..., ::-1]
    stream_flow, stream_metric = (
        padded(conserved, (("gx", 3),), 3, False),
        padded(metrics, (("gx", 3),), 3, False),
    )
    normal_flow, normal_metric = (
        padded(conserved, (("gy", 2),), 3, False),
        padded(metrics, (("gy", 2),), 3, False),
    )
    span_flow, span_metric = (
        padded(conserved, (("gz", 1),), 3, True),
        padded(metrics, (("gz", 1),), 3, True),
    )
    stream_row = stream_metric[0:3]
    normal_row = normal_metric[3:6]
    span_row = span_metric[6:9]
    stream_flow = fix_ends(stream_flow, at_inflow, at_outflow)
    stream_row = fix_ends(stream_row, at_inflow, at_outflow)
    momentum_sign = jnp.array([1.0, -1.0, -1.0, -1.0, 1.0], dtype=jnp.float32)[:, None, None, None]
    is_wake = wake_donor >= 0
    wake_flow = jnp.where(is_wake, mirrored[0:5], conserved[:, :, 2::-1, :] * momentum_sign)
    wake_row = jnp.where(is_wake, mirrored[5:8], metrics[3:6, :, 2::-1, :])
    normal_flow = fix_wall(normal_flow, wake_flow, at_wall, at_top)
    normal_row = fix_wall(normal_row, wake_row, at_wall, at_top)
    summed = divergence(stream_flow, stream_row, -1, 1)
    summed = summed + divergence(normal_flow, normal_row, -2, 2)
    summed = summed + divergence(span_flow, span_row, -3, 0)
    time_rate = -inv_volume[None] * summed
    return (conserved + STEP_SIZE * time_rate, time_rate)


def solution(mesh):
    placed = (P(None, "gz", "gy", "gx"), P(None, "gz", "gy", "gx"), P("gz", "gy", "gx"), P("gx"))
    return jax.shard_map(
        local,
        mesh=mesh,
        in_specs=placed,
        out_specs=(P(None, "gz", "gy", "gx"), P(None, "gz", "gy", "gx")),
        check_vma=False,
    )
```

profile of v0, /device:TPU:58, one launch (start us, length us, event | category | flops | bytes accessed | tf_op | source)
XLA Modules:
  0.0 86.0 jit_solution(15369266607397241721)
XLA Ops:
  0.6 1.0 %fusion.195 = (f32[5,4,8,3]{3,2,1,0:T(8,128)S(1)}, f32[5,4,8,3]{3,2,1,0:T(8,128)S(1)}) fusion(f32[5,4,8,128]{3,2,1,0:T(8,128)} %param.5), kind=kLoop, calls=%fused_computation.685 | loop fusion | bytes 7680 | tf_op jit(solution)/shard_map/slice | solution.py:25
  1.7 2.4 %collective-permute-start.1 = (f32[5,4,8,3]{3,2,1,0:T(8,128)S(1)}, f32[5,4,8,3]{3,2,1,0:T(8,128)S(1)}, u32[]{:S(2)}, u32[]{:S(2)}) collective-permute-start(f32[5,4,8,3]{3,2,1,0:T(8,128)S(1)} %get-tuple-element.353), channel_id=1, source_target_pairs={{192,0},{384,192},{576,384},{193,1},{385,193},{577,385},{194,2},{3... | collective-permute-start | bytes 5768 | tf_op jit(solution)/shard_map/ppermute | solution.py:25
  4.2 3.5 %collective-permute-start = (f32[5,4,8,3]{3,2,1,0:T(8,128)S(1)}, f32[5,4,8,3]{3,2,1,0:T(8,128)S(1)}, u32[]{:S(2)}, u32[]{:S(2)}) collective-permute-start(f32[5,4,8,3]{3,2,1,0:T(8,128)S(1)} %get-tuple-element.354), channel_id=1, source_target_pairs={{0,192},{192,384},{384,576},{1,193},{193,385},{385,577},{2,194},{1... | collective-permute-start | bytes 5768 | tf_op jit(solution)/shard_map/ppermute | solution.py:22
  7.7 0.1 fusion.191
  7.8 2.4 %collective-permute-start.3 = (f32[9,4,8,3]{3,2,1,0:T(8,128)S(1)}, f32[9,4,8,3]{3,2,1,0:T(8,128)S(1)}, u32[]{:S(2)}, u32[]{:S(2)}) collective-permute-start(f32[9,4,8,3]{3,2,1,0:T(8,128)S(1)} %get-tuple-element.329), channel_id=1, source_target_pairs={{192,0},{384,192},{576,384},{193,1},{385,193},{577,385},{194,2},{3... | collective-permute-start | bytes 10376 | tf_op jit(solution)/shard_map/ppermute | solution.py:25
  10.3 3.4 %collective-permute-start.2 = (f32[9,4,8,3]{3,2,1,0:T(8,128)S(1)}, f32[9,4,8,3]{3,2,1,0:T(8,128)S(1)}, u32[]{:S(2)}, u32[]{:S(2)}) collective-permute-start(f32[9,4,8,3]{3,2,1,0:T(8,128)S(1)} %get-tuple-element.328), channel_id=1, source_target_pairs={{0,192},{192,384},{384,576},{1,193},{193,385},{385,577},{2,194},{1... | collective-permute-start | bytes 10376 | tf_op jit(solution)/shard_map/ppermute | solution.py:22
  13.7 1.3 %collective-permute-start.7 = (f32[5,4,3,128]{3,2,1,0:T(4,128)S(1)}, f32[5,4,3,128]{3,2,1,0:T(4,128)S(1)}, u32[]{:S(2)}, u32[]{:S(2)}) collective-permute-start(f32[5,4,3,128]{3,2,1,0:T(4,128)S(1)} %get-tuple-element.355), channel_id=1, source_target_pairs={{16,0},{32,16},{48,32},{64,48},{80,64},{96,80},{112,96},{128,112},... | collective-permute-start | bytes 92168 | tf_op jit(solution)/shard_map/ppermute | solution.py:25
  15.0 0.2 slice_reduce_fusion.1
  15.2 0.2 slice_reduce_fusion.3
  15.6 0.6 copy-done.4
  16.3 0.7 copy-done.2
  17.0 2.4 %collective-permute-start.4 = (f32[8,4,3,128]{3,2,1,0:T(4,128)S(1)}, f32[8,4,3,128]{3,2,1,0:T(4,128)S(1)}, u32[]{:S(2)}, u32[]{:S(2)}) collective-permute-start(f32[8,4,3,128]{3,2,1,0:T(4,128)S(1)} %pad_maximum_fusion.11), channel_id=1, source_target_pairs={{0,192},{192,0},{384,576},{576,384},{1,193},{193,1},{385,577},{577... | collective-permute-start | bytes 147464 | tf_op jit(solution)/shard_map/ppermute | solution.py:12
  19.4 0.1 broadcast_select_fusion
  19.5 2.8 %collective-permute-start.6 = (f32[5,4,3,128]{3,2,1,0:T(4,128)S(1)}, f32[5,4,3,128]{3,2,1,0:T(4,128)S(1)}, u32[]{:S(2)}, u32[]{:S(2)}) collective-permute-start(f32[5,4,3,128]{3,2,1,0:T(4,128)S(1)} %get-tuple-element.356), channel_id=1, source_target_pairs={{0,16},{16,32},{32,48},{48,64},{64,80},{80,96},{96,112},{112,128},... | collective-permute-start | bytes 92168 | tf_op jit(solution)/shard_map/ppermute | solution.py:22
  22.3 0.1 broadcast_select_fusion.1
  22.4 0.1 pad_maximum_fusion.1
  22.5 4.2 %collective-permute-start.8 = (f32[9,4,3,128]{3,2,1,0:T(4,128)S(1)}, f32[9,4,3,128]{3,2,1,0:T(4,128)S(1)}, u32[]{:S(2)}, u32[]{:S(2)}) collective-permute-start(f32[9,4,3,128]{3,2,1,0:T(4,128)S(1)} %get-tuple-element.332), channel_id=1, source_target_pairs={{0,16},{16,32},{32,48},{48,64},{64,80},{80,96},{96,112},{112,128},... | collective-permute-start | bytes 165896 | tf_op jit(solution)/shard_map/ppermute | solution.py:22
  26.7 0.1 slice_select_fusion
  26.8 1.3 %collective-permute-start.9 = (f32[9,4,3,128]{3,2,1,0:T(4,128)S(1)}, f32[9,4,3,128]{3,2,1,0:T(4,128)S(1)}, u32[]{:S(2)}, u32[]{:S(2)}) collective-permute-start(f32[9,4,3,128]{3,2,1,0:T(4,128)S(1)} %get-tuple-element.333), channel_id=1, source_target_pairs={{16,0},{32,16},{48,32},{64,48},{80,64},{96,80},{112,96},{128,112},... | collective-permute-start | bytes 165896 | tf_op jit(solution)/shard_map/ppermute | solution.py:25
  28.1 0.1 slice_select_fusion.1
  28.2 0.1 fusion.15
  28.3 0.1 multiply_reduce_fusion.6
  28.5 0.1 fusion.1
  28.6 0.1 constant_dynamic-update-slice_fusion.9
  28.8 0.1 constant_dynamic-update-slice_fusion.29
  28.9 0.1 constant_dynamic-update-slice_fusion.49
  29.1 0.1 constant_dynamic-update-slice_fusion.19
  29.2 0.1 constant_dynamic-update-slice_fusion.59
  29.4 0.2 constant_dynamic-update-slice_fusion.44
  29.5 0.1 constant_dynamic-update-slice_fusion.4
  29.6 0.2 constant_dynamic-update-slice_fusion.24
  29.8 0.1 slice_maximum_fusion.5
  30.6 0.2 constant_dynamic-update-slice_fusion.43
  30.8 0.1 constant_dynamic-update-slice_fusion.3
  30.9 0.2 constant_dynamic-update-slice_fusion.52
  31.1 0.1 constant_dynamic-update-slice_fusion.2
  31.2 0.1 constant_dynamic-update-slice_fusion.1
  31.3 0.1 constant_dynamic-update-slice_fusion
  31.4 0.2 constant_dynamic-update-slice_fusion.41
  31.6 0.2 constant_dynamic-update-slice_fusion.40
  31.8 0.2 constant_dynamic-update-slice_fusion.23
  31.9 0.2 constant_dynamic-update-slice_fusion.22
  32.1 0.2 constant_dynamic-update-slice_fusion.21
  32.2 0.2 constant_dynamic-update-slice_fusion.20
  32.4 0.8 divide_add_fusion.1
  33.4 14.0 %collective-permute-start.10 = (f32[5,3,8,128]{3,2,1,0:T(8,128)S(1)}, f32[5,3,8,128]{3,2,1,0:T(8,128)S(1)}, u32[]{:S(2)}, u32[]{:S(2)}) collective-permute-start(f32[5,3,8,128]{3,2,1,0:T(8,128)S(1)} %get-tuple-element.361), channel_id=1, source_target_pairs={{0,1},{1,2},{2,3},{3,4},{4,5},{5,6},{6,7},{7,8},{8,9},{9,10},{10,1... | collective-permute-start | bytes 184328 | tf_op jit(solution)/shard_map/ppermute | solution.py:22
  47.5 1.9 %collective-permute-start.11 = (f32[5,3,8,128]{3,2,1,0:T(8,128)S(1)}, f32[5,3,8,128]{3,2,1,0:T(8,128)S(1)}, u32[]{:S(2)}, u32[]{:S(2)}) collective-permute-start(f32[5,3,8,128]{3,2,1,0:T(8,128)S(1)} %get-tuple-element.360), channel_id=1, source_target_pairs={{1,0},{2,1},{3,2},{4,3},{5,4},{6,5},{7,6},{8,7},{9,8},{10,9},{11,1... | collective-permute-start | bytes 184328 | tf_op jit(solution)/shard_map/ppermute | solution.py:25
  49.5 2.2 %collective-permute-done.10 = f32[5,3,8,128]{3,2,1,0:T(8,128)S(1)} collective-permute-done((f32[5,3,8,128]{3,2,1,0:T(8,128)S(1)}, f32[5,3,8,128]{3,2,1,0:T(8,128)S(1)}, u32[]{:S(2)}, u32[]{:S(2)}) %collective-permute-start.10) | collective-permute-done | bytes 61472 | tf_op jit(solution)/shard_map/ppermute | solution.py:22
  51.6 12.8 %collective-permute-start.12 = (f32[9,3,8,128]{3,2,1,0:T(8,128)S(1)}, f32[9,3,8,128]{3,2,1,0:T(8,128)S(1)}, u32[]{:S(2)}, u32[]{:S(2)}) collective-permute-start(f32[9,3,8,128]{3,2,1,0:T(8,128)S(1)} %get-tuple-element.335), channel_id=1, source_target_pairs={{0,1},{1,2},{2,3},{3,4},{4,5},{5,6},{6,7},{7,8},{8,9},{9,10},{10,1... | collective-permute-start | bytes 331784 | tf_op jit(solution)/shard_map/ppermute | solution.py:22
  64.5 1.9 %collective-permute-start.13 = (f32[9,3,8,128]{3,2,1,0:T(8,128)S(1)}, f32[9,3,8,128]{3,2,1,0:T(8,128)S(1)}, u32[]{:S(2)}, u32[]{:S(2)}) collective-permute-start(f32[9,3,8,128]{3,2,1,0:T(8,128)S(1)} %get-tuple-element.334), channel_id=1, source_target_pairs={{1,0},{2,1},{3,2},{4,3},{5,4},{6,5},{7,6},{8,7},{9,8},{10,9},{11,1... | collective-permute-start | bytes 331784 | tf_op jit(solution)/shard_map/ppermute | solution.py:25
  66.4 2.9 %collective-permute-start.5 = (f32[8,4,3,128]{3,2,1,0:T(4,128)S(1)}, f32[8,4,3,128]{3,2,1,0:T(4,128)S(1)}, u32[]{:S(2)}, u32[]{:S(2)}) collective-permute-start(f32[8,4,3,128]{3,2,1,0:T(4,128)S(1)} %collective-permute-done.4), channel_id=1, source_target_pairs={{0,384},{192,576},{384,0},{576,192},{1,385},{193,577},{385,1},{577... | collective-permute-start | bytes 147464 | tf_op jit(solution)/shard_map/ppermute | solution.py:12
  69.3 4.8 %collective-permute-done.5 = f32[8,4,3,128]{3,2,1,0:T(4,128)S(1)} collective-permute-done((f32[8,4,3,128]{3,2,1,0:T(4,128)S(1)}, f32[8,4,3,128]{3,2,1,0:T(4,128)S(1)}, u32[]{:S(2)}, u32[]{:S(2)}) %collective-permute-start.5) | collective-permute-done | bytes 49184 | tf_op jit(solution)/shard_map/ppermute | solution.py:12
  74.1 0.1 slice.1065
  74.2 0.5 copy-done.3
  74.7 0.1 select_select_fusion
  74.9 0.1 slice.1080
  75.2 0.1 constant_dynamic-update-slice_fusion.74
  76.5 0.1 constant_dynamic-update-slice_fusion.108
  77.0 0.1 constant_dynamic-update-slice_fusion.88
  77.2 0.8 divide_add_fusion
  78.3 4.8 %collective-permute-done.13 = f32[9,3,8,128]{3,2,1,0:T(8,128)S(1)} collective-permute-done((f32[9,3,8,128]{3,2,1,0:T(8,128)S(1)}, f32[9,3,8,128]{3,2,1,0:T(8,128)S(1)}, u32[]{:S(2)}, u32[]{:S(2)}) %collective-permute-start.13) | collective-permute-done | bytes 110624 | tf_op jit(solution)/shard_map/ppermute | solution.py:25
  83.3 0.1 constant_dynamic-update-slice_fusion.147
  84.5 0.5 divide_add_fusion.2
  85.2 0.8 multiply_add_fusion
  (166 shorter events, 4.6 us)
Async XLA Ops:
  0.6 7.1 %copy-start.1 = (f32[9,4,8,128]{3,2,1,0:T(8,128)S(1)}, f32[9,4,8,128]{3,2,1,0:T(8,128)}, u32[]{:S(2)}) copy-start(f32[9,4,8,128]{3,2,1,0:T(8,128)} %param.6) | copy-start | bytes 442372
  1.7 15.3 %collective-permute-start.1 = (f32[5,4,8,3]{3,2,1,0:T(8,128)S(1)}, f32[5,4,8,3]{3,2,1,0:T(8,128)S(1)}, u32[]{:S(2)}, u32[]{:S(2)}) collective-permute-start(f32[5,4,8,3]{3,2,1,0:T(8,128)S(1)} %get-tuple-element.353), channel_id=1, source_target_pairs={{192,0},{384,192},{576,384},{193,1},{385,193},{577,385},{194,2},{3... | collective-permute-start | bytes 5768 | tf_op jit(solution)/shard_map/ppermute | solution.py:25
  4.1 9.5 %copy-start = (f32[5,4,8,128]{3,2,1,0:T(8,128)S(1)}, f32[5,4,8,128]{3,2,1,0:T(8,128)}, u32[]{:S(2)}) copy-start(f32[5,4,8,128]{3,2,1,0:T(8,128)} %param.5) | copy-start | bytes 245764
  4.2 15.3 %collective-permute-start = (f32[5,4,8,3]{3,2,1,0:T(8,128)S(1)}, f32[5,4,8,3]{3,2,1,0:T(8,128)S(1)}, u32[]{:S(2)}, u32[]{:S(2)}) collective-permute-start(f32[5,4,8,3]{3,2,1,0:T(8,128)S(1)} %get-tuple-element.354), channel_id=1, source_target_pairs={{0,192},{192,384},{384,576},{1,193},{193,385},{385,577},{2,194},{1... | collective-permute-start | bytes 5768 | tf_op jit(solution)/shard_map/ppermute | solution.py:22
  7.8 14.7 %collective-permute-start.3 = (f32[9,4,8,3]{3,2,1,0:T(8,128)S(1)}, f32[9,4,8,3]{3,2,1,0:T(8,128)S(1)}, u32[]{:S(2)}, u32[]{:S(2)}) collective-permute-start(f32[9,4,8,3]{3,2,1,0:T(8,128)S(1)} %get-tuple-element.329), channel_id=1, source_target_pairs={{192,0},{384,192},{576,384},{193,1},{385,193},{577,385},{194,2},{3... | collective-permute-start | bytes 10376 | tf_op jit(solution)/shard_map/ppermute | solution.py:25
  10.3 16.5 %collective-permute-start.2 = (f32[9,4,8,3]{3,2,1,0:T(8,128)S(1)}, f32[9,4,8,3]{3,2,1,0:T(8,128)S(1)}, u32[]{:S(2)}, u32[]{:S(2)}) collective-permute-start(f32[9,4,8,3]{3,2,1,0:T(8,128)S(1)} %get-tuple-element.328), channel_id=1, source_target_pairs={{0,192},{192,384},{384,576},{1,193},{193,385},{385,577},{2,194},{1... | collective-permute-start | bytes 10376 | tf_op jit(solution)/shard_map/ppermute | solution.py:22
  13.7 19.7 %collective-permute-start.7 = (f32[5,4,3,128]{3,2,1,0:T(4,128)S(1)}, f32[5,4,3,128]{3,2,1,0:T(4,128)S(1)}, u32[]{:S(2)}, u32[]{:S(2)}) collective-permute-start(f32[5,4,3,128]{3,2,1,0:T(4,128)S(1)} %get-tuple-element.355), channel_id=1, source_target_pairs={{16,0},{32,16},{48,32},{64,48},{80,64},{96,80},{112,96},{128,112},... | collective-permute-start | bytes 92168 | tf_op jit(solution)/shard_map/ppermute | solution.py:25
  15.5 0.7 copy-start.4
  16.2 0.7 copy-start.2
  17.0 47.5 %collective-permute-start.4 = (f32[8,4,3,128]{3,2,1,0:T(4,128)S(1)}, f32[8,4,3,128]{3,2,1,0:T(4,128)S(1)}, u32[]{:S(2)}, u32[]{:S(2)}) collective-permute-start(f32[8,4,3,128]{3,2,1,0:T(4,128)S(1)} %pad_maximum_fusion.11), channel_id=1, source_target_pairs={{0,192},{192,0},{384,576},{576,384},{1,193},{193,1},{385,577},{577... | collective-permute-start | bytes 147464 | tf_op jit(solution)/shard_map/ppermute | solution.py:12
  19.5 54.7 %collective-permute-start.6 = (f32[5,4,3,128]{3,2,1,0:T(4,128)S(1)}, f32[5,4,3,128]{3,2,1,0:T(4,128)S(1)}, u32[]{:S(2)}, u32[]{:S(2)}) collective-permute-start(f32[5,4,3,128]{3,2,1,0:T(4,128)S(1)} %get-tuple-element.356), channel_id=1, source_target_pairs={{0,16},{16,32},{32,48},{48,64},{64,80},{80,96},{96,112},{112,128},... | collective-permute-start | bytes 92168 | tf_op jit(solution)/shard_map/ppermute | solution.py:22
  22.5 52.5 %collective-permute-start.8 = (f32[9,4,3,128]{3,2,1,0:T(4,128)S(1)}, f32[9,4,3,128]{3,2,1,0:T(4,128)S(1)}, u32[]{:S(2)}, u32[]{:S(2)}) collective-permute-start(f32[9,4,3,128]{3,2,1,0:T(4,128)S(1)} %get-tuple-element.332), channel_id=1, source_target_pairs={{0,16},{16,32},{32,48},{48,64},{64,80},{80,96},{96,112},{112,128},... | collective-permute-start | bytes 165896 | tf_op jit(solution)/shard_map/ppermute | solution.py:22
  26.8 20.7 %collective-permute-start.9 = (f32[9,4,3,128]{3,2,1,0:T(4,128)S(1)}, f32[9,4,3,128]{3,2,1,0:T(4,128)S(1)}, u32[]{:S(2)}, u32[]{:S(2)}) collective-permute-start(f32[9,4,3,128]{3,2,1,0:T(4,128)S(1)} %get-tuple-element.333), channel_id=1, source_target_pairs={{16,0},{32,16},{48,32},{64,48},{80,64},{96,80},{112,96},{128,112},... | collective-permute-start | bytes 165896 | tf_op jit(solution)/shard_map/ppermute | solution.py:25
  33.4 18.2 %collective-permute-start.10 = (f32[5,3,8,128]{3,2,1,0:T(8,128)S(1)}, f32[5,3,8,128]{3,2,1,0:T(8,128)S(1)}, u32[]{:S(2)}, u32[]{:S(2)}) collective-permute-start(f32[5,3,8,128]{3,2,1,0:T(8,128)S(1)} %get-tuple-element.361), channel_id=1, source_target_pairs={{0,1},{1,2},{2,3},{3,4},{4,5},{5,6},{6,7},{7,8},{8,9},{9,10},{10,1... | collective-permute-start | bytes 184328 | tf_op jit(solution)/shard_map/ppermute | solution.py:22
  47.5 18.9 %collective-permute-start.11 = (f32[5,3,8,128]{3,2,1,0:T(8,128)S(1)}, f32[5,3,8,128]{3,2,1,0:T(8,128)S(1)}, u32[]{:S(2)}, u32[]{:S(2)}) collective-permute-start(f32[5,3,8,128]{3,2,1,0:T(8,128)S(1)} %get-tuple-element.360), channel_id=1, source_target_pairs={{1,0},{2,1},{3,2},{4,3},{5,4},{6,5},{7,6},{8,7},{9,8},{10,9},{11,1... | collective-permute-start | bytes 184328 | tf_op jit(solution)/shard_map/ppermute | solution.py:25
  51.6 26.6 %collective-permute-start.12 = (f32[9,3,8,128]{3,2,1,0:T(8,128)S(1)}, f32[9,3,8,128]{3,2,1,0:T(8,128)S(1)}, u32[]{:S(2)}, u32[]{:S(2)}) collective-permute-start(f32[9,3,8,128]{3,2,1,0:T(8,128)S(1)} %get-tuple-element.335), channel_id=1, source_target_pairs={{0,1},{1,2},{2,3},{3,4},{4,5},{5,6},{6,7},{7,8},{8,9},{9,10},{10,1... | collective-permute-start | bytes 331784 | tf_op jit(solution)/shard_map/ppermute | solution.py:22
  64.5 18.7 %collective-permute-start.13 = (f32[9,3,8,128]{3,2,1,0:T(8,128)S(1)}, f32[9,3,8,128]{3,2,1,0:T(8,128)S(1)}, u32[]{:S(2)}, u32[]{:S(2)}) collective-permute-start(f32[9,3,8,128]{3,2,1,0:T(8,128)S(1)} %get-tuple-element.334), channel_id=1, source_target_pairs={{1,0},{2,1},{3,2},{4,3},{5,4},{6,5},{7,6},{8,7},{9,8},{10,9},{11,1... | collective-permute-start | bytes 331784 | tf_op jit(solution)/shard_map/ppermute | solution.py:25
  66.4 7.7 %collective-permute-start.5 = (f32[8,4,3,128]{3,2,1,0:T(4,128)S(1)}, f32[8,4,3,128]{3,2,1,0:T(4,128)S(1)}, u32[]{:S(2)}, u32[]{:S(2)}) collective-permute-start(f32[8,4,3,128]{3,2,1,0:T(4,128)S(1)} %collective-permute-done.4), channel_id=1, source_target_pairs={{0,384},{192,576},{384,0},{576,192},{1,385},{193,577},{385,1},{577... | collective-permute-start | bytes 147464 | tf_op jit(solution)/shard_map/ppermute | solution.py:12
  74.1 0.7 copy-start.3
where the time goes:
time: 86.5 us; the launch traced here: 86 us
  starting transfers between devices  57.3 us (66%)
  waiting for transfers between devices  11.8 us (14%)
  other arithmetic  11.2 us (13%)
  local copies, waits for them, and re-layouts  3.83 us (4%)
  between operations  1.79 us (2%)
    ppermute x6, starting transfers between devices, padded(): lax.ppermute(lax.slice_in_dim(block, block.shape[dim] - width, None, axis...  40.7 us
    ppermute x6, starting transfers between devices, padded(): lax.ppermute(lax.slice_in_dim(block, 0, width, axis=dim), axis, backward)  11.3 us
    unnamed x100, other arithmetic  5.44 us
    ppermute x2, starting transfers between devices, from_partner(): lax.ppermute(x, axis, [(i, i ^ 1 << bit) for i in range(lax.axis_size(axi...  5.31 us
    ppermute x6, waiting for transfers between devices, padded(): lax.ppermute(lax.slice_in_dim(block, 0, width, axis=dim), axis, backward)  4.85 us
    ppermute x2, waiting for transfers between devices, from_partner(): lax.ppermute(x, axis, [(i, i ^ 1 << bit) for i in range(lax.axis_size(axi...  4.76 us
    add x3, other arithmetic, interface_flux(): combined = weno_side(upwind[0:5]) + weno_side(downwind[5:0:-1])  2.2 us
    ppermute x6, waiting for transfers between devices, padded(): lax.ppermute(lax.slice_in_dim(block, block.shape[dim] - width, None, axis...  2.16 us
  transfers between devices with their start and end apart: 14, of which 3 were waited for; matrix products, arithmetic and copies ran while one was open for 11% of the time, Pallas kernels for 0%

commit v1 on v0

v1 whole, which is shorter than its diff:
```python
import jax
import jax.numpy as jnp
from jax import lax
from jax.experimental import pallas as pl
from jax.experimental.pallas import tpu as pltpu
from jax.sharding import PartitionSpec as P

GAMMA = 1.4
WENO_EPS = 1e-06
STEP_SIZE = 0.08
MESH = pl.DeviceIdType.MESH

XL, XH, YL, YH, ZL, ZH, MIR = range(7)
FLUX, SPEED, VEL, PRES, ROW = 5, 10, 11, 14, 15
CELL_ROWS = 18


def order_of(direction):
    return [direction % 3, (direction + 1) % 3, (direction + 2) % 3]


def cell_terms(fields, row):
    inverse = 1.0 / fields[0]
    velocity = [fields[1 + member] * inverse for member in range(3)]
    kinetic = 0.5 * sum(fields[1 + member] * velocity[member] for member in range(3))
    pressure = (GAMMA - 1.0) * (fields[4] - kinetic)
    contra = sum(row[member] * velocity[member] for member in range(3))
    fluxes = [fields[0] * contra]
    fluxes += [fields[1 + member] * contra + row[member] * pressure for member in range(3)]
    fluxes += [(fields[4] + pressure) * contra]
    size = sum(row[member] * row[member] for member in range(3))
    speed = jnp.abs(contra) + jnp.sqrt(GAMMA * pressure * inverse * size)
    return fluxes, speed, velocity, pressure


def weno_shift(d1, d2, d3, d4):
    s0, s1, s2 = d2 - d1, d3 - d2, d4 - d3
    q2 = d2 * d2 + WENO_EPS
    q3 = d3 * d3 + WENO_EPS
    b0 = s0 * ((4.0 / 3.0) * s0 + d2) + q2
    b1 = s1 * ((4.0 / 3.0) * s1 + d2) + q2
    b2 = s2 * ((4.0 / 3.0) * s2 - d3) + q3
    p01, p02, p12 = b0 * b1, b0 * b2, b1 * b2
    w0 = p12 * p12
    w1 = 6.0 * (p02 * p02)
    w2 = 3.0 * (p01 * p01)
    g0 = 2.0 * s0 + 3.0 * d2
    g1 = d2 + 2.0 * d3
    g2 = 3.0 * d3 - s2
    return (w0 * g0 + w1 * g1 + w2 * g2) / (w0 + w1 + w2)


def face_flux(get):
    alpha = get(SPEED, 0)
    for cell in range(1, 6):
        alpha = jnp.maximum(alpha, get(SPEED, cell))
    rho = 0.5 * (get(0, 2) + get(0, 3))
    ua, ub, uc = [0.5 * (get(VEL + m, 2) + get(VEL + m, 3)) for m in range(3)]
    pressure = 0.5 * (get(PRES, 2) + get(PRES, 3))
    sa, sb, sc = [get(ROW + m, 2) + get(ROW + m, 3) for m in range(3)]
    flat = sa * sa + sc * sc
    inv_flat = lax.rsqrt(flat)
    inv_size = lax.rsqrt(flat + sb * sb)
    na, nb, nc = sa * inv_size, sb * inv_size, sc * inv_size
    la, lc = -sc * inv_flat, sa * inv_flat
    ma, mb, mc = nb * lc, nc * la - na * lc, -nb * la
    c2 = GAMMA * pressure / rho
    ic = lax.rsqrt(c2)
    c = c2 * ic
    f = (GAMMA - 1.0) * ic * ic
    kinetic = 0.5 * (ua * ua + ub * ub + uc * uc)
    q = na * ua + nb * ub + nc * uc
    a = la * ua + lc * uc
    b = ma * ua + mb * ub + mc * uc
    f4 = 0.25 * f
    g4 = f4 * kinetic
    fa, fb, fc = f4 * ua, f4 * ub, f4 * uc
    i4 = 0.25 * ic
    q4, ia, ib, jc = i4 * q, i4 * na, i4 * nb, i4 * nc
    la2, lc2, a2 = 0.5 * la, 0.5 * lc, 0.5 * a
    ma2, mb2, mc2, b2 = 0.5 * ma, 0.5 * mb, 0.5 * mc, 0.5 * b

    def left(v):
        s = g4 * v[0] - (fa * v[1] + fb * v[2] + fc * v[3]) + f4 * v[4]
        t = q4 * v[0] - (ia * v[1] + ib * v[2] + jc * v[3])
        return [
            s + t,
            0.5 * v[0] - 2.0 * s,
            la2 * v[1] + lc2 * v[3] - a2 * v[0],
            ma2 * v[1] + mb2 * v[2] + mc2 * v[3] - b2 * v[0],
            s - t,
        ]

    up, down, middle = [], [], None
    for step in range(5):
        dq = [get(m, step + 1) - get(m, step) for m in range(5)]
        dg = [get(FLUX + m, step + 1) - get(FLUX + m, step) for m in range(5)]
        aq = [alpha * dq[m] for m in range(5)]
        if step < 4:
            up.append(left([dg[m] + aq[m] for m in range(5)]))
        if step > 0:
            down.append(left([dg[m] - aq[m] for m in range(5)]))
        if step == 2:
            middle = [0.5 * (get(FLUX + m, 2) + get(FLUX + m, 3) - aq[m]) for m in range(5)]
    chars = []
    for m in range(5):
        plus = weno_shift(up[0][m], up[1][m], up[2][m], up[3][m])
        minus = weno_shift(down[3][m], down[2][m], down[1][m], down[0][m])
        chars.append((1.0 / 6.0) * (plus - minus))
    ends = chars[0] + chars[4]
    total = ends + chars[1]
    along = c * (chars[4] - chars[0])
    energy = kinetic * total + (1.0 / (GAMMA - 1.0)) * c2 * ends + q * along + a * chars[2] + b * chars[3]
    return [
        middle[0] + total,
        middle[1] + (ua * total + na * along + la * chars[2] + ma * chars[3]),
        middle[2] + (ub * total + nb * along + mb * chars[3]),
        middle[3] + (uc * total + nc * along + lc * chars[2] + mc * chars[3]),
        middle[4] + energy,
    ]


def reversed_lanes(value):
    lane = lax.broadcasted_iota(jnp.int32, value.shape, 1)
    for bit in range(7):
        step = 1 << bit
        value = jnp.where((lane & step) == 0, pltpu.roll(value, 128 - step, 1), pltpu.roll(value, step, 1))
    return value


def kernel(
    q_hbm, s_hbm, inv_hbm, wake_hbm, rate_out, state_out,
    qv, sv, iv, wv, xl, xh, yl, yh, zl, zh, mir, ex, exh, ey, ez, fx, fy, fz, acc,
    send_sem, recv_sem, own_sem, far_in, row_in, go,
):
    gx, gy, gz = lax.axis_index("gx"), lax.axis_index("gy"), lax.axis_index("gz")
    y = lax.rem(gz, 8)
    late = gz >= 8
    edge_low, edge_high = y == 0, y == 7
    edge = jnp.logical_or(edge_low, edge_high)
    far_late = jnp.logical_and(late, edge)
    far_early = jnp.logical_and(jnp.logical_not(late), edge)
    beside_far = jnp.logical_and(late, jnp.logical_or(y == 1, y == 6))
    wall, top = gy == 0, gy == 11
    inflow, outflow = gx == 0, gx == 3
    not_ = jnp.logical_not
    both = jnp.logical_and

    up_z = (gx, gy, lax.rem(gz + 1, 16))
    down_z = (gx, gy, lax.rem(gz + 15, 16))
    partner = (gx, gy, jnp.where(edge_low, down_z[2], up_z[2]))
    inner = (gx, gy, jnp.where(edge_low, up_z[2], down_z[2]))
    outer = (gx, gy, jnp.where(y == 1, down_z[2], up_z[2]))
    row = [
        (not_(inflow), (gx - 1, gy, gz)),
        (not_(outflow), (gx + 1, gy, gz)),
        (not_(wall), (gx, gy - 1, gz)),
        (not_(top), (gx, gy + 1, gz)),
        (both(wall, jnp.logical_or(inflow, outflow)), (3 - gx, gy, gz)),
    ]
    spans = [(not_(edge_high), up_z, y + 1), (not_(edge_low), down_z, y - 1)]
    barrier = pltpu.get_barrier_semaphore()

    def signal(semaphore, target):
        pl.semaphore_signal(semaphore, inc=1, device_id=target, device_id_type=MESH)

    buffers = (xl, xh, yl, yh, zl, zh, mir)

    def copies(slot):
        target = {
            XL: (gx + 1, gy, gz),
            XH: (gx - 1, gy, gz),
            YL: (gx, gy + 1, gz),
            YH: (gx, gy - 1, gz),
            ZL: up_z,
            ZH: down_z,
            MIR: (3 - gx, gy, gz),
        }[slot]
        direction = {XL: 0, XH: 0, YL: 1, YH: 1, ZL: 2, ZH: 2, MIR: 1}[slot]
        low, amount = {ZL: (1, 3), ZH: (0, 3)}.get(slot, (0, 4))
        pieces = [
            (q_hbm.at[:, pl.ds(low, amount)], buffers[slot].at[pl.ds(0, 5)]),
            (s_hbm.at[pl.ds(3 * direction, 3), pl.ds(low, amount)], buffers[slot].at[pl.ds(5, 3)]),
        ]
        return [
            pltpu.make_async_remote_copy(
                src_ref=source,
                dst_ref=landing,
                send_sem=send_sem.at[slot, piece],
                recv_sem=recv_sem.at[slot, piece],
                device_id=target,
                device_id_type=MESH,
            )
            for piece, (source, landing) in enumerate(pieces)
        ]

    @pl.when(far_early)
    def _():
        signal(barrier, partner)

    @pl.when(far_late)
    def _():
        signal(barrier, inner)

    @pl.when(not_(far_late))
    def _():
        for there, target in row:
            @pl.when(there)
            def _():
                signal(barrier, target)
        for there, target, row_of in spans:
            target_far_late = both(late, jnp.logical_or(row_of == 0, row_of == 7))

            @pl.when(both(there, not_(target_far_late)))
            def _():
                signal(barrier, target)

    near_row = sum(there.astype(jnp.int32) for there, _ in row)
    near_span = sum(there.astype(jnp.int32) for there, _, _ in spans)
    pl.semaphore_wait(barrier, jnp.where(far_late, 1, near_row + near_span))

    def send_far():
        @pl.when(edge_high)
        def _():
            for copy in copies(ZL):
                copy.start()

        @pl.when(edge_low)
        def _():
            for copy in copies(ZH):
                copy.start()

    @pl.when(far_late)
    def _():
        send_far()
        signal(far_in, partner)

    own = [
        pltpu.make_async_copy(q_hbm, qv, own_sem.at[0]),
        pltpu.make_async_copy(s_hbm, sv, own_sem.at[1]),
        pltpu.make_async_copy(inv_hbm, iv, own_sem.at[2]),
        pltpu.make_async_copy(wake_hbm, wv, own_sem.at[3]),
    ]
    for copy in own:
        copy.start()

    @pl.when(far_late)
    def _():
        pl.semaphore_wait(go, 1)

    sends = [
        (XL, not_(outflow)),
        (XH, not_(inflow)),
        (YL, not_(top)),
        (YH, not_(wall)),
        (MIR, wall),
        (ZL, not_(edge_high)),
        (ZH, not_(edge_low)),
    ]
    for slot, there in sends:
        @pl.when(there)
        def _():
            for copy in copies(slot):
                copy.start()

    @pl.when(beside_far)
    def _():
        for there, target in row:
            @pl.when(there)
            def _():
                signal(row_in, target)
        pl.semaphore_wait(row_in, near_row)
        signal(go, outer)

    for copy in own:
        copy.wait()

    def arrive(slot):
        for copy in copies(slot):
            copy.wait_recv()

    lane = lax.broadcasted_iota(jnp.int32, (8, 128), 1)

    def fill(array, index):
        fields = [array[(m,) + index] for m in range(5)]
        metric = [array[(ROW + m,) + index] for m in range(3)]
        fluxes, speed, velocity, pressure = cell_terms(fields, metric)
        for m in range(5):
            array[(FLUX + m,) + index] = fluxes[m]
        array[(SPEED,) + index] = speed
        for m in range(3):
            array[(VEL + m,) + index] = velocity[m]
        array[(PRES,) + index] = pressure

    def raw_rows(direction):
        cyclic = order_of(direction)
        listed = [(0, 0, None), (4, 4, None)]
        for m in range(3):
            listed.append((1 + m, 1 + cyclic[m], None))
            listed.append((ROW + m, None, cyclic[m]))
        return listed

    @pl.when(not_(inflow))
    def _():
        arrive(XL)

    @pl.when(inflow)
    def _():
        for k in range(4):
            for f in range(5):
                xl[f, k] = jnp.broadcast_to(qv[f, k, :, 0:1], (8, 128))
            for f in range(3):
                xl[5 + f, k] = jnp.broadcast_to(sv[f, k, :, 0:1], (8, 128))

    @pl.when(not_(outflow))
    def _():
        arrive(XH)

    @pl.when(outflow)
    def _():
        for k in range(4):
            for f in range(5):
                xh[f, k] = jnp.broadcast_to(qv[f, k, :, 127:128], (8, 128))
            for f in range(3):
                xh[5 + f, k] = jnp.broadcast_to(sv[f, k, :, 127:128], (8, 128))

    for out, flow, metric in raw_rows(0):
        halo = flow if flow is not None else 5 + metric
        packed = None
        for k in range(4):
            centre = qv[flow, k] if flow is not None else sv[metric, k]
            ring = jnp.where(lane < 64, xh[halo, k], xl[halo, k])
            ex[out, k] = centre
            exh[out, k] = ring
            moved = pltpu.roll(jnp.where(lane < 64, ring, centre), (32 * k + 3) % 128, 1)
            packed = moved if packed is None else jnp.where(lane < 32 * k, packed, moved)
        ex[out, 4] = packed
        exh[out, 4] = packed

    def fill_x(k, carry):
        fill(ex, (k,))
        fill(exh, (k,))
        return carry

    lax.fori_loop(0, 5, fill_x, 0)

    def face_x(k, carry):
        cache = {}

        def get(r, cell):
            if (r, cell) not in cache:
                shift = 3 - cell
                centre = ex[r, k]
                if shift > 0:
                    centre = pltpu.roll(jnp.where(lane >= 128 - shift, exh[r, k], centre), shift, 1)
                elif shift < 0:
                    centre = pltpu.roll(jnp.where(lane < -shift, exh[r, k], centre), 128 + shift, 1)
                cache[(r, cell)] = centre
            return cache[(r, cell)]

        flux = face_flux(get)
        for m in range(5):
            fx[m, k] = flux[m]
        return carry

    lax.fori_loop(0, 5, face_x, 0)
    for k in range(4):
        for m in range(5):
            upper = pltpu.roll(fx[m, k], 127, 1)
            last = pltpu.roll(fx[m, 4], (124 - 32 * k) % 128, 1)
            acc[m, k] = jnp.where(lane == 127, last, upper) - fx[m, k]

    @pl.when(wall)
    def _():
        arrive(MIR)
        is_wake = jnp.broadcast_to(wv[0:1, :], (8, 128)) >= 0
        for f in range(8):
            for k in range(4):
                mirrored = reversed_lanes(mir[f, k])
                beside = qv[f, k] if f < 5 else sv[f - 2, k]
                if f in (1, 2, 3):
                    beside = -beside
                ghost = jnp.where(is_wake, mirrored, beside)
                for g in range(3):
                    yl[f, k, 7 - g : 8 - g, :] = ghost[g : g + 1, :]

    @pl.when(not_(wall))
    def _():
        arrive(YL)

    @pl.when(top)
    def _():
        for f in range(8):
            for k in range(4):
                source = qv[f, k, 7:8, :] if f < 5 else sv[f - 2, k, 7:8, :]
                yh[f, k] = jnp.broadcast_to(source, (8, 128))

    @pl.when(not_(top))
    def _():
        arrive(YH)

    for out, flow, metric in raw_rows(1):
        halo = flow if flow is not None else 5 + metric
        for k in range(4):
            base = 14 * k
            ey[out, base : base + 3, :] = yl[halo, k, 5:8, :]
            ey[out, base + 3 : base + 11, :] = qv[flow, k] if flow is not None else sv[3 + metric, k]
            ey[out, base + 11 : base + 14, :] = yh[halo, k, 0:3, :]
        ey[out, 56:64, :] = qv[flow, 3] if flow is not None else sv[3 + metric, 3]

    def fill_y(k, carry):
        fill(ey, (pl.ds(pl.multiple_of(8 * k, 8), 8),))
        return carry

    lax.fori_loop(0, 8, fill_y, 0)

    def face_y(k, carry):
        cache = {}

        def get(r, cell):
            if (r, cell) not in cache:
                cache[(r, cell)] = ey[r, pl.ds(8 * k + cell, 8), :]
            return cache[(r, cell)]

        flux = face_flux(get)
        for m in range(5):
            fy[m, pl.ds(pl.multiple_of(8 * k, 8), 8), :] = flux[m]
        return carry

    lax.fori_loop(0, 7, face_y, 0)
    cyclic = order_of(1)
    for k in range(4):
        for m in range(5):
            target = 1 + cyclic[m - 1] if 1 <= m <= 3 else m
            acc[target, k] += fy[m, 14 * k + 1 : 14 * k + 9, :] - fy[m, 14 * k : 14 * k + 8, :]

    def fill_z(first, last):
        def body(k, carry):
            fill(ez, (k,))
            return carry

        lax.fori_loop(first, last, body, 0)

    def take_z(halo_ref, base):
        for out, flow, metric in raw_rows(2):
            halo = flow if flow is not None else 5 + metric
            for k in range(3):
                ez[out, base + k] = halo_ref[halo, k]

    def face_z(k, carry):
        cache = {}

        def get(r, cell):
            if (r, cell) not in cache:
                cache[(r, cell)] = ez[r, k + cell]
            return cache[(r, cell)]

        flux = face_flux(get)
        for m in range(5):
            fz[m, k] = flux[m]
        return carry

    for out, flow, metric in raw_rows(2):
        for k in range(4):
            ez[out, 3 + k] = qv[flow, k] if flow is not None else sv[6 + metric, k]
    fill_z(3, 7)

    def low_z():
        arrive(ZL)
        take_z(zl, 0)
        fill_z(0, 3)

    def high_z():
        arrive(ZH)
        take_z(zh, 7)
        fill_z(7, 10)

    @pl.when(not_(edge_low))
    def _():
        low_z()

    @pl.when(not_(edge_high))
    def _():
        high_z()

    early_first = jnp.where(edge_low, 3, 0)
    early_last = jnp.where(edge_low, 5, jnp.where(edge_high, 2, 5))
    lax.fori_loop(early_first, early_last, face_z, 0)

    @pl.when(far_early)
    def _():
        pl.semaphore_wait(far_in, 1)
        send_far()

    @pl.when(edge_low)
    def _():
        low_z()

    @pl.when(edge_high)
    def _():
        high_z()

    late_first = jnp.where(edge_high, 2, 0)
    late_last = jnp.where(edge_low, 3, jnp.where(edge_high, 5, 0))
    lax.fori_loop(late_first, late_last, face_z, 0)

    cyclic = order_of(2)
    for m in range(5):
        target = 1 + cyclic[m - 1] if 1 <= m <= 3 else m
        for k in range(4):
            rate = -iv[k] * (acc[target, k] + (fz[m, k + 1] - fz[m, k]))
            rate_out[target, k] = rate
            state_out[target, k] = qv[target, k] + STEP_SIZE * rate

    for slot, there in sends:
        @pl.when(jnp.logical_or(there, edge if slot in (ZL, ZH) else there))
        def _():
            for copy in copies(slot):
                copy.wait_send()


def local(conserved, metrics, inv_volume, wake_donor):
    block = conserved.shape
    planes, rows, lanes = block[1:]
    wide = jax.ShapeDtypeStruct(block, jnp.float32)
    f32 = lambda *shape: pltpu.VMEM(shape, jnp.float32)
    rate, state = pl.pallas_call(
        kernel,
        out_shape=(wide, wide),
        in_specs=[pl.BlockSpec(memory_space=pltpu.HBM)] * 4,
        out_specs=[pl.BlockSpec(memory_space=pltpu.VMEM)] * 2,
        scratch_shapes=[
            f32(*block),
            f32(9, planes, rows, lanes),
            f32(planes, rows, lanes),
            pltpu.VMEM((1, lanes), jnp.int32),
            *[f32(8, planes, rows, lanes)] * 4,
            *[f32(8, 3, rows, lanes)] * 2,
            f32(8, planes, rows, lanes),
            f32(CELL_ROWS, 5, rows, lanes),
            f32(CELL_ROWS, 5, rows, lanes),
            f32(CELL_ROWS, 64, lanes),
            f32(CELL_ROWS, 10, rows, lanes),
            f32(5, 5, rows, lanes),
            f32(5, 56, lanes),
            f32(5, 5, rows, lanes),
            f32(*block),
            pltpu.SemaphoreType.DMA((7, 2)),
            pltpu.SemaphoreType.DMA((7, 2)),
            pltpu.SemaphoreType.DMA((4,)),
            pltpu.SemaphoreType.REGULAR,
            pltpu.SemaphoreType.REGULAR,
            pltpu.SemaphoreType.REGULAR,
        ],
        compiler_params=pltpu.CompilerParams(collective_id=0, has_side_effects=True),
    )(conserved, metrics, inv_volume, wake_donor[None])
    return state, rate


def solution(mesh):
    placed = (P(None, "gz", "gy", "gx"), P(None, "gz", "gy", "gx"), P("gz", "gy", "gx"), P("gx"))
    return jax.shard_map(
        local,
        mesh=mesh,
        in_specs=placed,
        out_specs=(P(None, "gz", "gy", "gx"), P(None, "gz", "gy", "gx")),
        check_vma=False,
    )
```

time: 86.5 us -> 27.8 us (0.32)
  the two profiles are of different devices: /device:TPU:58 before, /device:TPU:64 now
where the time goes in v1:
time: 27.8 us; the launch traced here: 27.6 us
  Pallas kernels  24.8 us (89%)
  local copies, waits for them, and re-layouts  2.2 us (8%)
  between operations  0.65 us (2%)
    pallas_call x1, Pallas kernels, local(): pl.pallas_call(kernel, out_shape=(wide, wide), in_specs=[pl.BlockSpec(mem...  24.8 us
    unnamed x4, local copies, waits for them, and re-layouts  2.2 us

profile of v1, /device:TPU:64, one launch (start us, length us, event | category | flops | bytes accessed | tf_op | source)
XLA Modules:
  0.0 27.6 jit_solution(6562413020739753003)
XLA Ops:
  0.6 24.8 %shard_map.59 = (f32[5,4,8,128]{3,2,1,0:T(8,128)}, f32[5,4,8,128]{3,2,1,0:T(8,128)}) custom-call(f32[5,4,8,128]{3,2,1,0:T(8,128)} %q_hbm.1, f32[9,4,8,128]{3,2,1,0:T(8,128)} %s_hbm.1, f32[4,8,128]{2,1,0:T(8,128)} %inv_hbm.1, s32[1,128]{1,0:T(1,128)} %bitcast.1), custom_call_target="tpu_custom_call" | custom-call | tf_op jit(solution)/shard_map/pallas_call | solution.py:527
  25.4 0.0 copy-start
  25.4 1.6 %copy.8 = f32[5,4,8,128]{3,2,1,0:T(8,128)} copy(f32[5,4,8,128]{3,2,1,0:T(8,128)} %get-tuple-element.8) | data formatting | bytes 163840
  27.0 0.0 copy-done
  27.0 0.6 %copy.9 = f32[5,4,8,128]{3,2,1,0:T(8,128)} copy(f32[5,4,8,128]{3,2,1,0:T(8,128)S(1)} %copy-done) | data formatting | bytes 163840
Async XLA Ops:
  25.4 1.6 %copy-start = (f32[5,4,8,128]{3,2,1,0:T(8,128)S(1)}, f32[5,4,8,128]{3,2,1,0:T(8,128)}, u32[]{:S(2)}) copy-start(f32[5,4,8,128]{3,2,1,0:T(8,128)} %get-tuple-element.9) | copy-start | bytes 245764

commit v2 on v1

--- a/solution.py
+++ b/solution.py
@@ -230,9 +230,14 @@
             for copy in copies(ZH):
                 copy.start()
 
+    rank = gy // 2
+
+    @pl.when(both(far_late, rank < 2))
+    def _():
+        send_far()
+
     @pl.when(far_late)
     def _():
-        send_far()
         signal(far_in, partner)
 
     own = [
@@ -244,9 +249,19 @@
     for copy in own:
         copy.start()
 
+    @pl.when(both(far_late, both(rank >= 2, rank < 4)))
+    def _():
+        own[0].wait()
+        own[1].wait()
+        send_far()
+
     @pl.when(far_late)
     def _():
         pl.semaphore_wait(go, 1)
+
+    @pl.when(both(far_late, rank >= 4))
+    def _():
+        send_far()
 
     sends = [
         (XL, not_(outflow)),
@@ -272,8 +287,13 @@
         pl.semaphore_wait(row_in, near_row)
         signal(go, outer)
 
-    for copy in own:
-        copy.wait()
+    @pl.when(not_(both(far_late, both(rank >= 2, rank < 4))))
+    def _():
+        own[0].wait()
+        own[1].wait()
+
+    own[2].wait()
+    own[3].wait()
 
     def arrive(slot):
         for copy in copies(slot):
@@ -519,10 +539,21 @@
                 copy.wait_send()
 
 
+def deliver(state, rate, state_out, rate_out, sem):
+    copies = [
+        pltpu.make_async_copy(state, state_out, sem.at[0]),
+        pltpu.make_async_copy(rate, rate_out, sem.at[1]),
+    ]
+    for copy in copies:
+        copy.start()
+    for copy in copies:
+        copy.wait()
+
+
 def local(conserved, metrics, inv_volume, wake_donor):
     block = conserved.shape
     planes, rows, lanes = block[1:]
-    wide = jax.ShapeDtypeStruct(block, jnp.float32)
+    wide = pltpu.VMEM(block, jnp.float32)
     f32 = lambda *shape: pltpu.VMEM(shape, jnp.float32)
     rate, state = pl.pallas_call(
         kernel,
@@ -554,7 +585,13 @@
         ],
         compiler_params=pltpu.CompilerParams(collective_id=0, has_side_effects=True),
     )(conserved, metrics, inv_volume, wake_donor[None])
-    return state, rate
+    return pl.pallas_call(
+        deliver,
+        out_shape=(jax.ShapeDtypeStruct(block, jnp.float32),) * 2,
+        in_specs=[pl.BlockSpec(memory_space=pl.ANY)] * 2,
+        out_specs=[pl.BlockSpec(memory_space=pltpu.HBM)] * 2,
+        scratch_shapes=[pltpu.SemaphoreType.DMA((2,))],
+    )(pltpu.with_memory_space_constraint(state, pltpu.VMEM), pltpu.with_memory_space_constraint(rate, pltpu.VMEM))
 
 
 def solution(mesh):

time: 27.8 us -> 24.5 us (0.88)
  the two profiles are of different devices: /device:TPU:64 before, /device:TPU:6 now
where the time goes in v2:
time: 24.5 us; the launch traced here: 24.1 us
  Pallas kernels  23.4 us (96%)
  between operations  0.64 us (3%)
    pallas_call x1, Pallas kernels, local(): pl.pallas_call(kernel, out_shape=(wide, wide), in_specs=[pl.BlockSpec(mem...  22.7 us
    pallas_call x1, Pallas kernels, local(): pl.pallas_call(deliver, out_shape=(jax.ShapeDtypeStruct(block, jnp.float3...  0.68 us

profile of v2, /device:TPU:6, one launch (start us, length us, event | category | flops | bytes accessed | tf_op | source)
XLA Modules:
  0.0 24.1 jit_solution(15271670963677642945)
XLA Ops:
  0.6 22.7 %shard_map.59 = (f32[5,4,8,128]{3,2,1,0:T(8,128)S(1)}, f32[5,4,8,128]{3,2,1,0:T(8,128)S(1)}) custom-call(f32[5,4,8,128]{3,2,1,0:T(8,128)} %q_hbm.1, f32[9,4,8,128]{3,2,1,0:T(8,128)} %s_hbm.1, f32[4,8,128]{2,1,0:T(8,128)} %inv_hbm.1, s32[1,128]{1,0:T(1,128)} %bitcast.1), custom_call_target="tpu_custom_call" | custom-call | tf_op jit(solution)/shard_map/pallas_call | solution.py:558
  23.4 0.7 %shard_map.60 = (f32[5,4,8,128]{3,2,1,0:T(8,128)}, f32[5,4,8,128]{3,2,1,0:T(8,128)}) custom-call(f32[5,4,8,128]{3,2,1,0:T(8,128)S(1)} %get-tuple-element.4.state, f32[5,4,8,128]{3,2,1,0:T(8,128)S(1)} %get-tuple-element.5.rate), custom_call_target="tpu_custom_call" | custom-call | tf_op jit(solution)/shard_map/pallas_call | solution.py:588

commit v3 on v2

--- a/solution.py
+++ b/solution.py
@@ -10,7 +10,7 @@
 STEP_SIZE = 0.08
 MESH = pl.DeviceIdType.MESH
 
-XL, XH, YL, YH, ZL, ZH, MIR = range(7)
+XL, XH, YL, YH, ZL, ZH, MIR, ZLX, ZHX, PASS = range(10)
 FLUX, SPEED, VEL, PRES, ROW = 5, 10, 11, 14, 15
 CELL_ROWS = 18
 
@@ -140,7 +140,15 @@
     edge = jnp.logical_or(edge_low, edge_high)
     far_late = jnp.logical_and(late, edge)
     far_early = jnp.logical_and(jnp.logical_not(late), edge)
-    beside_far = jnp.logical_and(late, jnp.logical_or(y == 1, y == 6))
+    beside = jnp.logical_or(y == 1, y == 6)
+    beside_far = jnp.logical_and(late, beside)
+    corner = jnp.logical_and(gx == 0, gy == 0)
+    lone, lone_far = jnp.logical_and(corner, gz == 0), jnp.logical_and(corner, gz == 15)
+    by_x, by_y, by_z, by_mirror = [
+        jnp.logical_and(jnp.logical_and(gx == i, gy == j), gz == k) for i, j, k in ((1, 0, 0), (0, 1, 0), (0, 0, 1), (3, 0, 0))
+    ]
+    adjacent = jnp.logical_or(jnp.logical_or(by_x, by_y), jnp.logical_or(by_z, by_mirror))
+    relay = jnp.logical_and(jnp.logical_and(gz < 8, beside), jnp.logical_not(jnp.logical_and(corner, gz == 1)))
     wall, top = gy == 0, gy == 11
     inflow, outflow = gx == 0, gx == 3
     not_ = jnp.logical_not
@@ -150,6 +158,7 @@
     down_z = (gx, gy, lax.rem(gz + 15, 16))
     partner = (gx, gy, jnp.where(edge_low, down_z[2], up_z[2]))
     inner = (gx, gy, jnp.where(edge_low, up_z[2], down_z[2]))
+    beyond = (gx, gy, jnp.where(jnp.logical_or(edge_low, y == 1), lax.rem(gz + 14, 16), lax.rem(gz + 2, 16)))
     outer = (gx, gy, jnp.where(y == 1, down_z[2], up_z[2]))
     row = [
         (not_(inflow), (gx - 1, gy, gz)),
@@ -164,7 +173,7 @@
     def signal(semaphore, target):
         pl.semaphore_signal(semaphore, inc=1, device_id=target, device_id_type=MESH)
 
-    buffers = (xl, xh, yl, yh, zl, zh, mir)
+    buffers = (xl, xh, yl, yh, zl, zh, mir, zl, zh)
 
     def copies(slot):
         target = {
@@ -175,12 +184,14 @@
             ZL: up_z,
             ZH: down_z,
             MIR: (3 - gx, gy, gz),
+            ZLX: up_z,
+            ZHX: down_z,
         }[slot]
-        direction = {XL: 0, XH: 0, YL: 1, YH: 1, ZL: 2, ZH: 2, MIR: 1}[slot]
-        low, amount = {ZL: (1, 3), ZH: (0, 3)}.get(slot, (0, 4))
+        direction = {XL: 0, XH: 0, YL: 1, YH: 1, MIR: 1}.get(slot, 2)
+        low, amount = {ZL: (1, 3), ZH: (0, 3), ZLX: (0, 1), ZHX: (3, 1)}.get(slot, (0, 4))
         pieces = [
-            (q_hbm.at[:, pl.ds(low, amount)], buffers[slot].at[pl.ds(0, 5)]),
-            (s_hbm.at[pl.ds(3 * direction, 3), pl.ds(low, amount)], buffers[slot].at[pl.ds(5, 3)]),
+            (q_hbm.at[:, pl.ds(low, amount)], buffers[slot].at[pl.ds(0, 5), pl.ds(low, amount)]),
+            (s_hbm.at[pl.ds(3 * direction, 3), pl.ds(low, amount)], buffers[slot].at[pl.ds(5, 3), pl.ds(low, amount)]),
         ]
         return [
             pltpu.make_async_remote_copy(
@@ -194,15 +205,33 @@
             for piece, (source, landing) in enumerate(pieces)
         ]
 
+    def passes(slot, held):
+        low = {ZL: 1, ZH: 0}[slot]
+        return [
+            pltpu.make_async_remote_copy(
+                src_ref=held.at[pl.ds(first, amount), pl.ds(low, 3)],
+                dst_ref=buffers[slot].at[pl.ds(first, amount), pl.ds(low, 3)],
+                send_sem=send_sem.at[PASS, piece],
+                recv_sem=recv_sem.at[slot, piece],
+                device_id=beyond,
+                device_id_type=MESH,
+            )
+            for piece, (first, amount) in enumerate(((0, 5), (5, 3)))
+        ]
+
     @pl.when(far_early)
     def _():
         signal(barrier, partner)
 
+    @pl.when(relay)
+    def _():
+        signal(barrier, beyond)
+
     @pl.when(far_late)
     def _():
         signal(barrier, inner)
 
-    @pl.when(not_(far_late))
+    @pl.when(not_(jnp.logical_or(far_late, lone)))
     def _():
         for there, target in row:
             @pl.when(there)
@@ -217,7 +246,7 @@
 
     near_row = sum(there.astype(jnp.int32) for there, _ in row)
     near_span = sum(there.astype(jnp.int32) for there, _, _ in spans)
-    pl.semaphore_wait(barrier, jnp.where(far_late, 1, near_row + near_span))
+    pl.semaphore_wait(barrier, jnp.where(lone_far, 1, jnp.where(far_late, 2, near_row + near_span - adjacent.astype(jnp.int32))))
 
     def send_far():
         @pl.when(edge_high)
@@ -230,15 +259,23 @@
             for copy in copies(ZH):
                 copy.start()
 
-    rank = gy // 2
-
-    @pl.when(both(far_late, rank < 2))
+    @pl.when(far_late)
+    def _():
+        signal(far_in, (gx, gy, jnp.where(lone_far, partner[2], beyond[2])))
+
+    turn = gy // 2
+
+    @pl.when(both(far_late, both(edge_high, turn == 3)))
+    def _():
+        pl.delay(1000)
+
+    @pl.when(both(far_late, both(edge_high, turn == 5)))
+    def _():
+        pl.delay(2000)
+
+    @pl.when(far_late)
     def _():
         send_far()
-
-    @pl.when(far_late)
-    def _():
-        signal(far_in, partner)
 
     own = [
         pltpu.make_async_copy(q_hbm, qv, own_sem.at[0]),
@@ -249,19 +286,9 @@
     for copy in own:
         copy.start()
 
-    @pl.when(both(far_late, both(rank >= 2, rank < 4)))
-    def _():
-        own[0].wait()
-        own[1].wait()
-        send_far()
-
     @pl.when(far_late)
     def _():
         pl.semaphore_wait(go, 1)
-
-    @pl.when(both(far_late, rank >= 4))
-    def _():
-        send_far()
 
     sends = [
         (XL, not_(outflow)),
@@ -271,12 +298,20 @@
         (MIR, wall),
         (ZL, not_(edge_high)),
         (ZH, not_(edge_low)),
+        (ZLX, both(both(edge_low, not_(late)), not_(lone))),
+        (ZHX, both(edge_high, not_(late))),
     ]
+    to_lone = {XH: by_x, YH: by_y, ZH: by_z, MIR: by_mirror}
     for slot, there in sends:
-        @pl.when(there)
+        @pl.when(both(there, not_(to_lone[slot])) if slot in to_lone else there)
         def _():
             for copy in copies(slot):
                 copy.start()
+
+    @pl.when(lone)
+    def _():
+        for target in ((1, 0, 0), (0, 1, 0), (0, 0, 1), (3, 0, 0)):
+            signal(row_in, target)
 
     @pl.when(beside_far)
     def _():
@@ -287,13 +322,8 @@
         pl.semaphore_wait(row_in, near_row)
         signal(go, outer)
 
-    @pl.when(not_(both(far_late, both(rank >= 2, rank < 4))))
-    def _():
-        own[0].wait()
-        own[1].wait()
-
-    own[2].wait()
-    own[3].wait()
+    for copy in own:
+        copy.wait()
 
     def arrive(slot):
         for copy in copies(slot):
@@ -319,6 +349,15 @@
             listed.append((1 + m, 1 + cyclic[m], None))
             listed.append((ROW + m, None, cyclic[m]))
         return listed
+
+    @pl.when(adjacent)
+    def _():
+        pl.semaphore_wait(row_in, 1)
+        for slot, there in to_lone.items():
+            @pl.when(there)
+            def _():
+                for copy in copies(slot):
+                    copy.start()
 
     @pl.when(not_(inflow))
     def _():
@@ -461,11 +500,11 @@
 
         lax.fori_loop(first, last, body, 0)
 
-    def take_z(halo_ref, base):
+    def take_z(halo_ref, base, low):
         for out, flow, metric in raw_rows(2):
             halo = flow if flow is not None else 5 + metric
             for k in range(3):
-                ez[out, base + k] = halo_ref[halo, k]
+                ez[out, base + k] = halo_ref[halo, low + k]
 
     def face_z(k, carry):
         cache = {}
@@ -487,12 +526,12 @@
 
     def low_z():
         arrive(ZL)
-        take_z(zl, 0)
+        take_z(zl, 0, 1)
         fill_z(0, 3)
 
     def high_z():
         arrive(ZH)
-        take_z(zh, 7)
+        take_z(zh, 7, 0)
         fill_z(7, 10)
 
     @pl.when(not_(edge_low))
@@ -507,7 +546,7 @@
     early_last = jnp.where(edge_low, 5, jnp.where(edge_high, 2, 5))
     lax.fori_loop(early_first, early_last, face_z, 0)
 
-    @pl.when(far_early)
+    @pl.when(lone)
     def _():
         pl.semaphore_wait(far_in, 1)
         send_far()
@@ -532,8 +571,27 @@
             rate_out[target, k] = rate
             state_out[target, k] = qv[target, k] + STEP_SIZE * rate
 
+    @pl.when(both(relay, y == 1))
+    def _():
+        arrive(ZLX)
+        pl.semaphore_wait(far_in, 1)
+        for copy in passes(ZH, zl):
+            copy.start()
+
+    @pl.when(both(relay, y == 6))
+    def _():
+        arrive(ZHX)
+        pl.semaphore_wait(far_in, 1)
+        for copy in passes(ZL, zh):
+            copy.start()
+
+    @pl.when(relay)
+    def _():
+        for copy in passes(ZH, zl):
+            copy.wait_send()
+
     for slot, there in sends:
-        @pl.when(jnp.logical_or(there, edge if slot in (ZL, ZH) else there))
+        @pl.when(jnp.logical_or(there, {ZL: far_late, ZH: jnp.logical_or(far_late, lone)}.get(slot, there)))
         def _():
             for copy in copies(slot):
                 copy.wait_send()
@@ -566,7 +624,7 @@
             f32(planes, rows, lanes),
             pltpu.VMEM((1, lanes), jnp.int32),
             *[f32(8, planes, rows, lanes)] * 4,
-            *[f32(8, 3, rows, lanes)] * 2,
+            *[f32(8, planes, rows, lanes)] * 2,
             f32(8, planes, rows, lanes),
             f32(CELL_ROWS, 5, rows, lanes),
             f32(CELL_ROWS, 5, rows, lanes),
@@ -576,8 +634,8 @@
             f32(5, 56, lanes),
             f32(5, 5, rows, lanes),
             f32(*block),
-            pltpu.SemaphoreType.DMA((7, 2)),
-            pltpu.SemaphoreType.DMA((7, 2)),
+            pltpu.SemaphoreType.DMA((10, 2)),
+            pltpu.SemaphoreType.DMA((10, 2)),
             pltpu.SemaphoreType.DMA((4,)),
             pltpu.SemaphoreType.REGULAR,
             pltpu.SemaphoreType.REGULAR,

time: 24.5 us -> 22.7 us (0.927)
  Pallas kernels: 23.4 us -> 21.9 us
    pallas_call x1, Pallas kernels: 22.7 us -> 21.2 us  [local(): pl.pallas_call(kernel, out_shape=(wide, wide), in_specs=[pl.BlockSpec(mem...]
where the time goes in v3:
time: 22.7 us; the launch traced here: 22.5 us
  Pallas kernels  21.9 us (96%)
  between operations  0.64 us (3%)
    pallas_call x1, Pallas kernels, local(): pl.pallas_call(kernel, out_shape=(wide, wide), in_specs=[pl.BlockSpec(mem...  21.2 us
    pallas_call x1, Pallas kernels, local(): pl.pallas_call(deliver, out_shape=(jax.ShapeDtypeStruct(block, jnp.float3...  0.68 us

profile of v3, /device:TPU:6, one launch (start us, length us, event | category | flops | bytes accessed | tf_op | source)
XLA Modules:
  0.0 22.5 jit_solution(164622407478693050)
XLA Ops:
  0.6 21.2 %shard_map.59 = (f32[5,4,8,128]{3,2,1,0:T(8,128)S(1)}, f32[5,4,8,128]{3,2,1,0:T(8,128)S(1)}) custom-call(f32[5,4,8,128]{3,2,1,0:T(8,128)} %q_hbm.1, f32[9,4,8,128]{3,2,1,0:T(8,128)} %s_hbm.1, f32[4,8,128]{2,1,0:T(8,128)} %inv_hbm.1, s32[1,128]{1,0:T(1,128)} %bitcast.1), custom_call_target="tpu_custom_call" | custom-call | tf_op jit(solution)/shard_map/pallas_call | solution.py:616
  21.8 0.7 %shard_map.60 = (f32[5,4,8,128]{3,2,1,0:T(8,128)}, f32[5,4,8,128]{3,2,1,0:T(8,128)}) custom-call(f32[5,4,8,128]{3,2,1,0:T(8,128)S(1)} %get-tuple-element.4.state, f32[5,4,8,128]{3,2,1,0:T(8,128)S(1)} %get-tuple-element.5.rate), custom_call_target="tpu_custom_call" | custom-call | tf_op jit(solution)/shard_map/pallas_call | solution.py:646

commit v4 on v3

--- a/solution.py
+++ b/solution.py
@@ -10,7 +10,7 @@
 STEP_SIZE = 0.08
 MESH = pl.DeviceIdType.MESH
 
-XL, XH, YL, YH, ZL, ZH, MIR, ZLX, ZHX, PASS = range(10)
+XL, XH, YL, YH, ZL, ZH, MIR, ZLX, ZHX = range(9)
 FLUX, SPEED, VEL, PRES, ROW = 5, 10, 11, 14, 15
 CELL_ROWS = 18
 
@@ -131,7 +131,7 @@
 def kernel(
     q_hbm, s_hbm, inv_hbm, wake_hbm, rate_out, state_out,
     qv, sv, iv, wv, xl, xh, yl, yh, zl, zh, mir, ex, exh, ey, ez, fx, fy, fz, acc,
-    send_sem, recv_sem, own_sem, far_in, row_in, go,
+    send_sem, recv_sem, own_sem, far_send, far_recv, far_in, row_in, go,
 ):
     gx, gy, gz = lax.axis_index("gx"), lax.axis_index("gy"), lax.axis_index("gz")
     y = lax.rem(gz, 8)
@@ -205,19 +205,81 @@
             for piece, (source, landing) in enumerate(pieces)
         ]
 
-    def passes(slot, held):
-        low = {ZL: 1, ZH: 0}[slot]
-        return [
-            pltpu.make_async_remote_copy(
-                src_ref=held.at[pl.ds(first, amount), pl.ds(low, 3)],
-                dst_ref=buffers[slot].at[pl.ds(first, amount), pl.ds(low, 3)],
-                send_sem=send_sem.at[PASS, piece],
-                recv_sem=recv_sem.at[slot, piece],
-                device_id=beyond,
-                device_id_type=MESH,
-            )
-            for piece, (first, amount) in enumerate(((0, 5), (5, 3)))
-        ]
+    def far_copies(slot, flow, metric, target):
+        listed = []
+        for stage in range(3):
+            plane = {ZL: 3 - stage, ZH: stage}[slot]
+            for source, landing in (
+                (flow.at[:, plane], buffers[slot].at[pl.ds(0, 5), plane]),
+                (metric.at[:, plane], buffers[slot].at[pl.ds(5, 3), plane]),
+            ):
+                listed.append(
+                    pltpu.make_async_remote_copy(
+                        src_ref=source,
+                        dst_ref=landing,
+                        send_sem=far_send,
+                        recv_sem=far_recv.at[stage],
+                        device_id=target,
+                        device_id_type=MESH,
+                    )
+                )
+        return listed
+
+    def far_arrive(slot, stage):
+        plane = 3 - stage if slot == ZL else stage
+        pltpu.make_async_remote_copy(
+            src_ref=buffers[slot].at[:, plane],
+            dst_ref=buffers[slot].at[:, plane],
+            send_sem=far_send,
+            recv_sem=far_recv.at[stage],
+            device_id=partner,
+            device_id_type=MESH,
+        ).wait_recv()
+
+    def far_sent():
+        pltpu.make_async_remote_copy(
+            src_ref=zl.at[:, pl.ds(0, 3)],
+            dst_ref=zl.at[:, pl.ds(0, 3)],
+            send_sem=far_send,
+            recv_sem=far_recv.at[0],
+            device_id=partner,
+            device_id_type=MESH,
+        ).wait_send()
+
+    def send_far():
+        flow, metric = q_hbm, s_hbm.at[pl.ds(6, 3)]
+
+        @pl.when(edge_high)
+        def _():
+            for copy in far_copies(ZL, flow, metric, partner):
+                copy.start()
+
+        @pl.when(edge_low)
+        def _():
+            for copy in far_copies(ZH, flow, metric, partner):
+                copy.start()
+
+    @pl.when(far_late)
+    def _():
+        pl.semaphore_wait(barrier, jnp.where(lone_far, 1, 2))
+
+    @pl.when(far_late)
+    def _():
+        signal(far_in, (gx, gy, jnp.where(lone_far, partner[2], beyond[2])))
+
+    turn = gy // 2
+
+    @pl.when(both(far_late, both(edge_high, turn == 3)))
+    def _():
+        pl.delay(1000)
+
+    @pl.when(both(far_late, both(edge_high, turn == 5)))
+    def _():
+        pl.delay(2000)
+
+    @pl.when(far_late)
+    def _():
+        send_far()
 
     @pl.when(far_early)
     def _():
@@ -246,36 +308,11 @@
 
     near_row = sum(there.astype(jnp.int32) for there, _ in row)
     near_span = sum(there.astype(jnp.int32) for there, _, _ in spans)
-    pl.semaphore_wait(barrier, jnp.where(lone_far, 1, jnp.where(far_late, 2, near_row + near_span - adjacent.astype(jnp.int32))))
-
-    def send_far():
-        @pl.when(edge_high)
-        def _():
-            for copy in copies(ZL):
-                copy.start()
-
-        @pl.when(edge_low)
-        def _():
-            for copy in copies(ZH):
-                copy.start()
-
-    @pl.when(far_late)
-    def _():
-        signal(far_in, (gx, gy, jnp.where(lone_far, partner[2], beyond[2])))
-
-    turn = gy // 2
-
-    @pl.when(both(far_late, both(edge_high, turn == 3)))
-    def _():
-        pl.delay(1000)
-
-    @pl.when(both(far_late, both(edge_high, turn == 5)))
-    def _():
-        pl.delay(2000)
-
-    @pl.when(far_late)
-    def _():
-        send_far()
+
+    @pl.when(not_(far_late))
+    def _():
+        pl.semaphore_wait(barrier, near_row + near_span - adjacent.astype(jnp.int32))
+
 
     own = [
         pltpu.make_async_copy(q_hbm, qv, own_sem.at[0]),
@@ -500,11 +537,14 @@
 
         lax.fori_loop(first, last, body, 0)
 
-    def take_z(halo_ref, base, low):
+    def take_plane(halo_ref, cell, plane):
         for out, flow, metric in raw_rows(2):
             halo = flow if flow is not None else 5 + metric
-            for k in range(3):
-                ez[out, base + k] = halo_ref[halo, low + k]
+            ez[out, cell] = halo_ref[halo, plane]
+
+    def take_z(halo_ref, base, low):
+        for k in range(3):
+            take_plane(halo_ref, base + k, low + k)
 
     def face_z(k, carry):
         cache = {}
@@ -551,17 +591,24 @@
         pl.semaphore_wait(far_in, 1)
         send_far()
 
-    @pl.when(edge_low)
-    def _():
-        low_z()
-
-    @pl.when(edge_high)
-    def _():
-        high_z()
-
-    late_first = jnp.where(edge_high, 2, 0)
-    late_last = jnp.where(edge_low, 3, jnp.where(edge_high, 5, 0))
-    lax.fori_loop(late_first, late_last, face_z, 0)
+    @pl.when(edge)
+    def _():
+        def body(stage, carry):
+            @pl.when(edge_low)
+            def _():
+                far_arrive(ZL, stage)
+                take_plane(zl, 2 - stage, 3 - stage)
+                fill(ez, (2 - stage,))
+
+            @pl.when(edge_high)
+            def _():
+                far_arrive(ZH, stage)
+                take_plane(zh, 7 + stage, stage)
+                fill(ez, (7 + stage,))
+
+            return face_z(jnp.where(edge_low, 2 - stage, 2 + stage), carry)
+
+        lax.fori_loop(0, 3, body, 0)
 
     cyclic = order_of(2)
     for m in range(5):
@@ -575,23 +622,22 @@
     def _():
         arrive(ZLX)
         pl.semaphore_wait(far_in, 1)
-        for copy in passes(ZH, zl):
+        for copy in far_copies(ZH, zl.at[pl.ds(0, 5)], zl.at[pl.ds(5, 3)], beyond):
             copy.start()
 
     @pl.when(both(relay, y == 6))
     def _():
         arrive(ZHX)
         pl.semaphore_wait(far_in, 1)
-        for copy in passes(ZL, zh):
+        for copy in far_copies(ZL, zh.at[pl.ds(0, 5)], zh.at[pl.ds(5, 3)], beyond):
             copy.start()
 
-    @pl.when(relay)
-    def _():
-        for copy in passes(ZH, zl):
-            copy.wait_send()
+    @pl.when(jnp.logical_or(relay, jnp.logical_or(far_late, lone)))
+    def _():
+        far_sent()
 
     for slot, there in sends:
-        @pl.when(jnp.logical_or(there, {ZL: far_late, ZH: jnp.logical_or(far_late, lone)}.get(slot, there)))
+        @pl.when(there)
         def _():
             for copy in copies(slot):
                 copy.wait_send()
@@ -634,9 +680,11 @@
             f32(5, 56, lanes),
             f32(5, 5, rows, lanes),
             f32(*block),
-            pltpu.SemaphoreType.DMA((10, 2)),
-            pltpu.SemaphoreType.DMA((10, 2)),
+            pltpu.SemaphoreType.DMA((9, 2)),
+            pltpu.SemaphoreType.DMA((9, 2)),
             pltpu.SemaphoreType.DMA((4,)),
+            pltpu.SemaphoreType.DMA,
+            pltpu.SemaphoreType.DMA((3,)),
             pltpu.SemaphoreType.REGULAR,
             pltpu.SemaphoreType.REGULAR,
             pltpu.SemaphoreType.REGULAR,

time: 22.7 us -> 22.3 us (0.982)
  Pallas kernels: 21.9 us -> 21.5 us
    pallas_call x1, Pallas kernels: 21.2 us -> 20.8 us  [local(): pl.pallas_call(kernel, out_shape=(wide, wide), in_specs=[pl.BlockSpec(mem...]
where the time goes in v4:
time: 22.3 us; the launch traced here: 22.1 us
  Pallas kernels  21.5 us (96%)
  between operations  0.64 us (3%)
    pallas_call x1, Pallas kernels, local(): pl.pallas_call(kernel, out_shape=(wide, wide), in_specs=[pl.BlockSpec(mem...  20.8 us
    pallas_call x1, Pallas kernels, local(): pl.pallas_call(deliver, out_shape=(jax.ShapeDtypeStruct(block, jnp.float3...  0.68 us

profile of v4, /device:TPU:6, one launch (start us, length us, event | category | flops | bytes accessed | tf_op | source)
XLA Modules:
  0.0 22.1 jit_solution(10286829840432050715)
XLA Ops:
  0.6 20.8 %shard_map.59 = (f32[5,4,8,128]{3,2,1,0:T(8,128)S(1)}, f32[5,4,8,128]{3,2,1,0:T(8,128)S(1)}) custom-call(f32[5,4,8,128]{3,2,1,0:T(8,128)} %q_hbm.1, f32[9,4,8,128]{3,2,1,0:T(8,128)} %s_hbm.1, f32[4,8,128]{2,1,0:T(8,128)} %inv_hbm.1, s32[1,128]{1,0:T(1,128)} %bitcast.1), custom_call_target="tpu_custom_call" | custom-call | tf_op jit(solution)/shard_map/pallas_call | solution.py:662
  21.4 0.7 %shard_map.60 = (f32[5,4,8,128]{3,2,1,0:T(8,128)}, f32[5,4,8,128]{3,2,1,0:T(8,128)}) custom-call(f32[5,4,8,128]{3,2,1,0:T(8,128)S(1)} %get-tuple-element.4.state, f32[5,4,8,128]{3,2,1,0:T(8,128)S(1)} %get-tuple-element.5.rate), custom_call_target="tpu_custom_call" | custom-call | tf_op jit(solution)/shard_map/pallas_call | solution.py:694

commit v5 on v4

--- a/solution.py
+++ b/solution.py
@@ -131,7 +131,7 @@
 def kernel(
     q_hbm, s_hbm, inv_hbm, wake_hbm, rate_out, state_out,
     qv, sv, iv, wv, xl, xh, yl, yh, zl, zh, mir, ex, exh, ey, ez, fx, fy, fz, acc,
-    send_sem, recv_sem, own_sem, far_send, far_recv, far_in, row_in, go,
+    send_sem, recv_sem, own_sem, far_send, far_recv, word,
 ):
     gx, gy, gz = lax.axis_index("gx"), lax.axis_index("gy"), lax.axis_index("gz")
     y = lax.rem(gz, 8)
@@ -197,12 +197,12 @@
             pltpu.make_async_remote_copy(
                 src_ref=source,
                 dst_ref=landing,
-                send_sem=send_sem.at[slot, piece],
-                recv_sem=recv_sem.at[slot, piece],
+                send_sem=send_sem.at[0 if slot in (XL, XH) else 1 if slot in (YL, YH, MIR) else 2],
+                recv_sem=recv_sem.at[{ZLX: ZL, ZHX: ZH}.get(slot, slot)],
                 device_id=target,
                 device_id_type=MESH,
             )
-            for piece, (source, landing) in enumerate(pieces)
+            for source, landing in pieces
         ]
 
     def far_copies(slot, flow, metric, target):
@@ -265,7 +265,7 @@
 
     @pl.when(far_late)
     def _():
-        signal(far_in, (gx, gy, jnp.where(lone_far, partner[2], beyond[2])))
+        signal(word, (gx, gy, jnp.where(lone_far, partner[2], beyond[2])))
 
     turn = gy // 2
 
@@ -316,16 +316,16 @@
 
     own = [
         pltpu.make_async_copy(q_hbm, qv, own_sem.at[0]),
-        pltpu.make_async_copy(s_hbm, sv, own_sem.at[1]),
-        pltpu.make_async_copy(inv_hbm, iv, own_sem.at[2]),
-        pltpu.make_async_copy(wake_hbm, wv, own_sem.at[3]),
+        pltpu.make_async_copy(s_hbm, sv, own_sem.at[0]),
+        pltpu.make_async_copy(inv_hbm, iv, own_sem.at[1]),
+        pltpu.make_async_copy(wake_hbm, wv, own_sem.at[2]),
     ]
     for copy in own:
         copy.start()
 
     @pl.when(far_late)
     def _():
-        pl.semaphore_wait(go, 1)
+        pl.semaphore_wait(word, 1)
 
     sends = [
         (XL, not_(outflow)),
@@ -348,23 +348,36 @@
     @pl.when(lone)
     def _():
         for target in ((1, 0, 0), (0, 1, 0), (0, 0, 1), (3, 0, 0)):
-            signal(row_in, target)
+            signal(word, target)
 
     @pl.when(beside_far)
     def _():
         for there, target in row:
             @pl.when(there)
             def _():
-                signal(row_in, target)
-        pl.semaphore_wait(row_in, near_row)
-        signal(go, outer)
-
-    for copy in own:
-        copy.wait()
-
-    def arrive(slot):
-        for copy in copies(slot):
-            copy.wait_recv()
+                signal(word, target)
+        pl.semaphore_wait(word, near_row)
+        signal(word, outer)
+
+    pltpu.make_async_copy(ex.at[pl.ds(0, 14), pl.ds(0, 4)], exh.at[pl.ds(0, 14), pl.ds(0, 4)], own_sem.at[0]).wait()
+    own[2].wait()
+    own[3].wait()
+
+    def awaited(ref, slot, group):
+        return pltpu.make_async_remote_copy(
+            src_ref=ref,
+            dst_ref=ref,
+            send_sem=send_sem.at[group],
+            recv_sem=recv_sem.at[slot],
+            device_id=up_z,
+            device_id_type=MESH,
+        )
+
+    def arrive(slot, low=0, amount=4):
+        awaited(buffers[slot].at[:, pl.ds(low, amount)], slot, 0).wait_recv()
+
+    def sent(group, fields, amount):
+        awaited(ex.at[pl.ds(0, fields), pl.ds(0, amount)], 0, group).wait_send()
 
     lane = lax.broadcasted_iota(jnp.int32, (8, 128), 1)
 
@@ -389,7 +402,7 @@
 
     @pl.when(adjacent)
     def _():
-        pl.semaphore_wait(row_in, 1)
+        pl.semaphore_wait(word, 1)
         for slot, there in to_lone.items():
             @pl.when(there)
             def _():
@@ -565,12 +578,30 @@
     fill_z(3, 7)
 
     def low_z():
-        arrive(ZL)
+        passing = both(relay, y == 1)
+
+        @pl.when(passing)
+        def _():
+            arrive(ZL)
+
+        @pl.when(not_(passing))
+        def _():
+            arrive(ZL, 1, 3)
+
         take_z(zl, 0, 1)
         fill_z(0, 3)
 
     def high_z():
-        arrive(ZH)
+        passing = both(relay, y == 6)
+
+        @pl.when(passing)
+        def _():
+            arrive(ZH)
+
+        @pl.when(not_(passing))
+        def _():
+            arrive(ZH, 0, 3)
+
         take_z(zh, 7, 0)
         fill_z(7, 10)
 
@@ -588,11 +619,41 @@
 
     @pl.when(lone)
     def _():
-        pl.semaphore_wait(far_in, 1)
+        pl.semaphore_wait(word, 1)
         send_far()
 
+    extra = both(edge, both(not_(late), not_(lone)))
+    for group, fields, amount, there in (
+        (0, 16, 4, not_(jnp.logical_or(inflow, outflow))),
+        (0, 8, 4, jnp.logical_or(inflow, outflow)),
+        (1, 16, 4, not_(top)),
+        (1, 8, 4, top),
+        (2, 16, 3, not_(edge)),
+        (2, 8, 4, extra),
+        (2, 8, 3, both(edge, not_(extra))),
+    ):
+        @pl.when(there)
+        def _():
+            sent(group, fields, amount)
+
+    spanwise = order_of(2)
+
+    def finish(k):
+        for m in range(5):
+            target = 1 + spanwise[m - 1] if 1 <= m <= 3 else m
+            rate = -iv[k] * (acc[target, k] + (fz[m, k + 1] - fz[m, k]))
+            rate_out[target, k] = rate
+            state_out[target, k] = qv[target, k] + STEP_SIZE * rate
+
+    @pl.when(not_(edge))
+    def _():
+        for k in range(4):
+            finish(k)
+
     @pl.when(edge)
     def _():
+        finish(jnp.where(edge_low, 3, 0))
+
         def body(stage, carry):
             @pl.when(edge_low)
             def _():
@@ -606,41 +667,36 @@
                 take_plane(zh, 7 + stage, stage)
                 fill(ez, (7 + stage,))
 
-            return face_z(jnp.where(edge_low, 2 - stage, 2 + stage), carry)
+            carry = face_z(jnp.where(edge_low, 2 - stage, 2 + stage), carry)
+            finish(jnp.where(edge_low, 2 - stage, 1 + stage))
+            return carry
 
         lax.fori_loop(0, 3, body, 0)
 
-    cyclic = order_of(2)
-    for m in range(5):
-        target = 1 + cyclic[m - 1] if 1 <= m <= 3 else m
-        for k in range(4):
-            rate = -iv[k] * (acc[target, k] + (fz[m, k + 1] - fz[m, k]))
-            rate_out[target, k] = rate
-            state_out[target, k] = qv[target, k] + STEP_SIZE * rate
-
     @pl.when(both(relay, y == 1))
     def _():
-        arrive(ZLX)
-        pl.semaphore_wait(far_in, 1)
+        pl.semaphore_wait(word, 1)
+
+        @pl.when(turn == 3)
+        def _():
+            pl.delay(1000)
+
+        @pl.when(turn == 5)
+        def _():
+            pl.delay(2000)
+
         for copy in far_copies(ZH, zl.at[pl.ds(0, 5)], zl.at[pl.ds(5, 3)], beyond):
             copy.start()
 
     @pl.when(both(relay, y == 6))
     def _():
-        arrive(ZHX)
-        pl.semaphore_wait(far_in, 1)
+        pl.semaphore_wait(word, 1)
         for copy in far_copies(ZL, zh.at[pl.ds(0, 5)], zh.at[pl.ds(5, 3)], beyond):
             copy.start()
 
     @pl.when(jnp.logical_or(relay, jnp.logical_or(far_late, lone)))
     def _():
         far_sent()
-
-    for slot, there in sends:
-        @pl.when(there)
-        def _():
-            for copy in copies(slot):
-                copy.wait_send()
 
 
 def deliver(state, rate, state_out, rate_out, sem):
@@ -680,13 +736,11 @@
             f32(5, 56, lanes),
             f32(5, 5, rows, lanes),
             f32(*block),
-            pltpu.SemaphoreType.DMA((9, 2)),
-            pltpu.SemaphoreType.DMA((9, 2)),
-            pltpu.SemaphoreType.DMA((4,)),
+            pltpu.SemaphoreType.DMA((3,)),
+            pltpu.SemaphoreType.DMA((7,)),
+            pltpu.SemaphoreType.DMA((3,)),
             pltpu.SemaphoreType.DMA,
             pltpu.SemaphoreType.DMA((3,)),
-            pltpu.SemaphoreType.REGULAR,
-            pltpu.SemaphoreType.REGULAR,
             pltpu.SemaphoreType.REGULAR,
         ],
         compiler_params=pltpu.CompilerParams(collective_id=0, has_side_effects=True),

time: 22.3 us -> 22 us (0.987)
  Pallas kernels: 21.5 us -> 21.2 us
    pallas_call x1, Pallas kernels: 20.8 us -> 20.5 us  [local(): pl.pallas_call(kernel, out_shape=(wide, wide), in_specs=[pl.BlockSpec(mem...]
where the time goes in v5:
time: 22 us; the launch traced here: 21.8 us
  Pallas kernels  21.2 us (96%)
  between operations  0.64 us (3%)
    pallas_call x1, Pallas kernels, local(): pl.pallas_call(kernel, out_shape=(wide, wide), in_specs=[pl.BlockSpec(mem...  20.5 us
    pallas_call x1, Pallas kernels, local(): pl.pallas_call(deliver, out_shape=(jax.ShapeDtypeStruct(block, jnp.float3...  0.68 us

profile of v5, /device:TPU:6, one launch (start us, length us, event | category | flops | bytes accessed | tf_op | source)
XLA Modules:
  0.0 21.8 jit_solution(9755764770544669385)
XLA Ops:
  0.6 20.5 %shard_map.59 = (f32[5,4,8,128]{3,2,1,0:T(8,128)S(1)}, f32[5,4,8,128]{3,2,1,0:T(8,128)S(1)}) custom-call(f32[5,4,8,128]{3,2,1,0:T(8,128)} %q_hbm.1, f32[9,4,8,128]{3,2,1,0:T(8,128)} %s_hbm.1, f32[4,8,128]{2,1,0:T(8,128)} %inv_hbm.1, s32[1,128]{1,0:T(1,128)} %bitcast.1), custom_call_target="tpu_custom_call" | custom-call | tf_op jit(solution)/shard_map/pallas_call | solution.py:718
  21.2 0.7 %shard_map.60 = (f32[5,4,8,128]{3,2,1,0:T(8,128)}, f32[5,4,8,128]{3,2,1,0:T(8,128)}) custom-call(f32[5,4,8,128]{3,2,1,0:T(8,128)S(1)} %get-tuple-element.4.state, f32[5,4,8,128]{3,2,1,0:T(8,128)S(1)} %get-tuple-element.5.rate), custom_call_target="tpu_custom_call" | custom-call | tf_op jit(solution)/shard_map/pallas_call | solution.py:748

commit v6 on v5

--- a/solution.py
+++ b/solution.py
@@ -175,6 +175,8 @@
 
     buffers = (xl, xh, yl, yh, zl, zh, mir, zl, zh)
 
+    direction_of = {XL: 0, XH: 0, YL: 1, YH: 1, MIR: 1, ZL: 2, ZH: 2, ZLX: 2, ZHX: 2}
+
     def copies(slot):
         target = {
             XL: (gx + 1, gy, gz),
@@ -187,7 +189,7 @@
             ZLX: up_z,
             ZHX: down_z,
         }[slot]
-        direction = {XL: 0, XH: 0, YL: 1, YH: 1, MIR: 1}.get(slot, 2)
+        direction = direction_of[slot]
         low, amount = {ZL: (1, 3), ZH: (0, 3), ZLX: (0, 1), ZHX: (3, 1)}.get(slot, (0, 4))
         pieces = [
             (q_hbm.at[:, pl.ds(low, amount)], buffers[slot].at[pl.ds(0, 5), pl.ds(low, amount)]),
@@ -197,8 +199,8 @@
             pltpu.make_async_remote_copy(
                 src_ref=source,
                 dst_ref=landing,
-                send_sem=send_sem.at[0 if slot in (XL, XH) else 1 if slot in (YL, YH, MIR) else 2],
-                recv_sem=recv_sem.at[{ZLX: ZL, ZHX: ZH}.get(slot, slot)],
+                send_sem=send_sem.at[direction_of[slot]],
+                recv_sem=recv_sem.at[direction_of[slot]],
                 device_id=target,
                 device_id_type=MESH,
             )
@@ -317,8 +319,8 @@
     own = [
         pltpu.make_async_copy(q_hbm, qv, own_sem.at[0]),
         pltpu.make_async_copy(s_hbm, sv, own_sem.at[0]),
-        pltpu.make_async_copy(inv_hbm, iv, own_sem.at[1]),
-        pltpu.make_async_copy(wake_hbm, wv, own_sem.at[2]),
+        pltpu.make_async_copy(inv_hbm, iv, own_sem.at[0]),
+        pltpu.make_async_copy(wake_hbm, wv, own_sem.at[1]),
     ]
     for copy in own:
         copy.start()
@@ -359,25 +361,25 @@
         pl.semaphore_wait(word, near_row)
         signal(word, outer)
 
-    pltpu.make_async_copy(ex.at[pl.ds(0, 14), pl.ds(0, 4)], exh.at[pl.ds(0, 14), pl.ds(0, 4)], own_sem.at[0]).wait()
-    own[2].wait()
+    pltpu.make_async_copy(ex.at[pl.ds(0, 15), pl.ds(0, 4)], exh.at[pl.ds(0, 15), pl.ds(0, 4)], own_sem.at[0]).wait()
     own[3].wait()
 
-    def awaited(ref, slot, group):
+    def all_of(direction, fields, amount):
+        ref = ex.at[pl.ds(0, fields), pl.ds(0, amount)]
         return pltpu.make_async_remote_copy(
             src_ref=ref,
             dst_ref=ref,
-            send_sem=send_sem.at[group],
-            recv_sem=recv_sem.at[slot],
+            send_sem=send_sem.at[direction],
+            recv_sem=recv_sem.at[direction],
             device_id=up_z,
             device_id_type=MESH,
         )
 
-    def arrive(slot, low=0, amount=4):
-        awaited(buffers[slot].at[:, pl.ds(low, amount)], slot, 0).wait_recv()
-
-    def sent(group, fields, amount):
-        awaited(ex.at[pl.ds(0, fields), pl.ds(0, amount)], 0, group).wait_send()
+    def arrive(direction, counts):
+        for fields, amount, there in counts:
+            @pl.when(there)
+            def _():
+                all_of(direction, fields, amount).wait_recv()
 
     lane = lax.broadcasted_iota(jnp.int32, (8, 128), 1)
 
@@ -409,9 +411,8 @@
                 for copy in copies(slot):
                     copy.start()
 
-    @pl.when(not_(inflow))
-    def _():
-        arrive(XL)
+    x_end = jnp.logical_or(inflow, outflow)
+    arrive(0, ((16, 4, not_(x_end)), (8, 4, x_end)))
 
     @pl.when(inflow)
     def _():
@@ -420,10 +421,6 @@
                 xl[f, k] = jnp.broadcast_to(qv[f, k, :, 0:1], (8, 128))
             for f in range(3):
                 xl[5 + f, k] = jnp.broadcast_to(sv[f, k, :, 0:1], (8, 128))
-
-    @pl.when(not_(outflow))
-    def _():
-        arrive(XH)
 
     @pl.when(outflow)
     def _():
@@ -479,9 +476,10 @@
             last = pltpu.roll(fx[m, 4], (124 - 32 * k) % 128, 1)
             acc[m, k] = jnp.where(lane == 127, last, upper) - fx[m, k]
 
+    arrive(1, ((16, 4, not_(top)), (8, 4, top)))
+
     @pl.when(wall)
     def _():
-        arrive(MIR)
         is_wake = jnp.broadcast_to(wv[0:1, :], (8, 128)) >= 0
         for f in range(8):
             for k in range(4):
@@ -493,20 +491,12 @@
                 for g in range(3):
                     yl[f, k, 7 - g : 8 - g, :] = ghost[g : g + 1, :]
 
-    @pl.when(not_(wall))
-    def _():
-        arrive(YL)
-
     @pl.when(top)
     def _():
         for f in range(8):
             for k in range(4):
                 source = qv[f, k, 7:8, :] if f < 5 else sv[f - 2, k, 7:8, :]
                 yh[f, k] = jnp.broadcast_to(source, (8, 128))
-
-    @pl.when(not_(top))
-    def _():
-        arrive(YH)
 
     for out, flow, metric in raw_rows(1):
         halo = flow if flow is not None else 5 + metric
@@ -578,32 +568,14 @@
     fill_z(3, 7)
 
     def low_z():
-        passing = both(relay, y == 1)
-
-        @pl.when(passing)
-        def _():
-            arrive(ZL)
-
-        @pl.when(not_(passing))
-        def _():
-            arrive(ZL, 1, 3)
-
         take_z(zl, 0, 1)
         fill_z(0, 3)
 
     def high_z():
-        passing = both(relay, y == 6)
-
-        @pl.when(passing)
-        def _():
-            arrive(ZH)
-
-        @pl.when(not_(passing))
-        def _():
-            arrive(ZH, 0, 3)
-
         take_z(zh, 7, 0)
         fill_z(7, 10)
+
+    arrive(2, ((14, 4, relay), (16, 3, not_(jnp.logical_or(relay, edge))), (8, 3, edge)))
 
     @pl.when(not_(edge_low))
     def _():
@@ -623,9 +595,9 @@
         send_far()
 
     extra = both(edge, both(not_(late), not_(lone)))
-    for group, fields, amount, there in (
-        (0, 16, 4, not_(jnp.logical_or(inflow, outflow))),
-        (0, 8, 4, jnp.logical_or(inflow, outflow)),
+    for direction, fields, amount, there in (
+        (0, 16, 4, not_(x_end)),
+        (0, 8, 4, x_end),
         (1, 16, 4, not_(top)),
         (1, 8, 4, top),
         (2, 16, 3, not_(edge)),
@@ -634,7 +606,7 @@
     ):
         @pl.when(there)
         def _():
-            sent(group, fields, amount)
+            all_of(direction, fields, amount).wait_send()
 
     spanwise = order_of(2)
 
@@ -700,13 +672,14 @@
 
 
 def deliver(state, rate, state_out, rate_out, sem):
-    copies = [
+    whole = [
         pltpu.make_async_copy(state, state_out, sem.at[0]),
         pltpu.make_async_copy(rate, rate_out, sem.at[1]),
     ]
-    for copy in copies:
-        copy.start()
-    for copy in copies:
+    for m in range(state.shape[0]):
+        pltpu.make_async_copy(state.at[m], state_out.at[m], sem.at[0]).start()
+        pltpu.make_async_copy(rate.at[m], rate_out.at[m], sem.at[1]).start()
+    for copy in whole:
         copy.wait()
 
 
@@ -737,8 +710,8 @@
             f32(5, 5, rows, lanes),
             f32(*block),
             pltpu.SemaphoreType.DMA((3,)),
-            pltpu.SemaphoreType.DMA((7,)),
             pltpu.SemaphoreType.DMA((3,)),
+            pltpu.SemaphoreType.DMA((2,)),
             pltpu.SemaphoreType.DMA,
             pltpu.SemaphoreType.DMA((3,)),
             pltpu.SemaphoreType.REGULAR,

time: 22 us -> 21.9 us (level)
  no operation moved by 1% of the time
where the time goes in v6:
time: 21.9 us; the launch traced here: 21.8 us
  Pallas kernels  21.1 us (96%)
  between operations  0.64 us (3%)
    pallas_call x1, Pallas kernels, local(): pl.pallas_call(kernel, out_shape=(wide, wide), in_specs=[pl.BlockSpec(mem...  20.5 us
    pallas_call x1, Pallas kernels, local(): pl.pallas_call(deliver, out_shape=(jax.ShapeDtypeStruct(block, jnp.float3...  0.67 us

profile of v6, /device:TPU:6, one launch (start us, length us, event | category | flops | bytes accessed | tf_op | source)
XLA Modules:
  0.0 21.8 jit_solution(7247969124463482671)
XLA Ops:
  0.6 20.5 %shard_map.59 = (f32[5,4,8,128]{3,2,1,0:T(8,128)S(1)}, f32[5,4,8,128]{3,2,1,0:T(8,128)S(1)}) custom-call(f32[5,4,8,128]{3,2,1,0:T(8,128)} %q_hbm.1, f32[9,4,8,128]{3,2,1,0:T(8,128)} %s_hbm.1, f32[4,8,128]{2,1,0:T(8,128)} %inv_hbm.1, s32[1,128]{1,0:T(1,128)} %bitcast.1), custom_call_target="tpu_custom_call" | custom-call | tf_op jit(solution)/shard_map/pallas_call | solution.py:691
  21.1 0.7 %shard_map.60 = (f32[5,4,8,128]{3,2,1,0:T(8,128)}, f32[5,4,8,128]{3,2,1,0:T(8,128)}) custom-call(f32[5,4,8,128]{3,2,1,0:T(8,128)S(1)} %get-tuple-element.4.state, f32[5,4,8,128]{3,2,1,0:T(8,128)S(1)} %get-tuple-element.5.rate), custom_call_target="tpu_custom_call" | custom-call | tf_op jit(solution)/shard_map/pallas_call | solution.py:721

commit v7 on v6

--- a/solution.py
+++ b/solution.py
@@ -130,7 +130,7 @@
 
 def kernel(
     q_hbm, s_hbm, inv_hbm, wake_hbm, rate_out, state_out,
-    qv, sv, iv, wv, xl, xh, yl, yh, zl, zh, mir, ex, exh, ey, ez, fx, fy, fz, acc,
+    qv, sv, iv, wv, xl, xh, yl, yh, zl, zh, mir, held, ex, exh, ey, ez, fx, fy, fz, acc,
     send_sem, recv_sem, own_sem, far_send, far_recv, word,
 ):
     gx, gy, gz = lax.axis_index("gx"), lax.axis_index("gy"), lax.axis_index("gz")
@@ -207,13 +207,14 @@
             for source, landing in pieces
         ]
 
-    def far_copies(slot, flow, metric, target):
+    def far_copies(slot, flow, metric, target, into=None, stages=(0, 1, 2)):
         listed = []
-        for stage in range(3):
+        into = buffers[slot] if into is None else into
+        for stage in stages:
             plane = {ZL: 3 - stage, ZH: stage}[slot]
             for source, landing in (
-                (flow.at[:, plane], buffers[slot].at[pl.ds(0, 5), plane]),
-                (metric.at[:, plane], buffers[slot].at[pl.ds(5, 3), plane]),
+                (flow.at[:, plane], into.at[pl.ds(0, 5), plane]),
+                (metric.at[:, plane], into.at[pl.ds(5, 3), plane]),
             ):
                 listed.append(
                     pltpu.make_async_remote_copy(
@@ -248,12 +249,22 @@
             device_id_type=MESH,
         ).wait_send()
 
+    turn = gy // 2
+    detour_from = both(both(late, edge_high), gy == 9)
+    detour_at = both(both(late, y == 6), gy == 9)
+    detour_to = both(both(not_(late), edge_low), gy == 9)
+
     def send_far():
         flow, metric = q_hbm, s_hbm.at[pl.ds(6, 3)]
 
-        @pl.when(edge_high)
+        @pl.when(both(edge_high, not_(detour_from)))
         def _():
             for copy in far_copies(ZL, flow, metric, partner):
+                copy.start()
+
+        @pl.when(detour_from)
+        def _():
+            for copy in far_copies(ZL, flow, metric, inner, held):
                 copy.start()
 
         @pl.when(edge_low)
@@ -269,8 +280,6 @@
     def _():
         signal(word, (gx, gy, jnp.where(lone_far, partner[2], beyond[2])))
 
-    turn = gy // 2
-
     @pl.when(both(far_late, both(edge_high, turn == 3)))
     def _():
         pl.delay(1000)
@@ -285,7 +294,11 @@
 
     @pl.when(far_early)
     def _():
-        signal(barrier, partner)
+        signal(barrier, (gx, gy, jnp.where(detour_to, lax.rem(gz + 14, 16), partner[2])))
+
+    @pl.when(detour_at)
+    def _():
+        signal(barrier, outer)
 
     @pl.when(relay)
     def _():
@@ -313,7 +326,7 @@
 
     @pl.when(not_(far_late))
     def _():
-        pl.semaphore_wait(barrier, near_row + near_span - adjacent.astype(jnp.int32))
+        pl.semaphore_wait(barrier, near_row + near_span - adjacent.astype(jnp.int32) + detour_at.astype(jnp.int32))
 
 
     own = [
@@ -358,6 +371,24 @@
             @pl.when(there)
             def _():
                 signal(word, target)
+
+    @pl.when(detour_at)
+    def _():
+        for stage in range(3):
+            landed = held.at[:, 3 - stage]
+            pltpu.make_async_remote_copy(
+                src_ref=landed,
+                dst_ref=landed,
+                send_sem=far_send,
+                recv_sem=far_recv.at[stage],
+                device_id=beyond,
+                device_id_type=MESH,
+            ).wait_recv()
+            for copy in far_copies(ZL, held.at[pl.ds(0, 5)], held.at[pl.ds(5, 3)], beyond, None, (stage,)):
+                copy.start()
+
+    @pl.when(beside_far)
+    def _():
         pl.semaphore_wait(word, near_row)
         signal(word, outer)
 
@@ -666,7 +697,7 @@
         for copy in far_copies(ZL, zh.at[pl.ds(0, 5)], zh.at[pl.ds(5, 3)], beyond):
             copy.start()
 
-    @pl.when(jnp.logical_or(relay, jnp.logical_or(far_late, lone)))
+    @pl.when(jnp.logical_or(jnp.logical_or(relay, detour_at), jnp.logical_or(far_late, lone)))
     def _():
         far_sent()
 
@@ -700,7 +731,7 @@
             pltpu.VMEM((1, lanes), jnp.int32),
             *[f32(8, planes, rows, lanes)] * 4,
             *[f32(8, planes, rows, lanes)] * 2,
-            f32(8, planes, rows, lanes),
+            *[f32(8, planes, rows, lanes)] * 2,
             f32(CELL_ROWS, 5, rows, lanes),
             f32(CELL_ROWS, 5, rows, lanes),
             f32(CELL_ROWS, 64, lanes),

time: 21.9 us -> 21.9 us (level)
  no operation moved by 1% of the time
where the time goes in v7:
time: 21.9 us; the launch traced here: 21.8 us
  Pallas kernels  21.1 us (96%)
  between operations  0.64 us (3%)
    pallas_call x1, Pallas kernels, local(): pl.pallas_call(kernel, out_shape=(wide, wide), in_specs=[pl.BlockSpec(mem...  20.5 us
    pallas_call x1, Pallas kernels, local(): pl.pallas_call(deliver, out_shape=(jax.ShapeDtypeStruct(block, jnp.float3...  0.67 us

profile of v7, /device:TPU:6, one launch (start us, length us, event | category | flops | bytes accessed | tf_op | source)
XLA Modules:
  0.0 21.8 jit_solution(13378577907006650148)
XLA Ops:
  0.6 20.5 %shard_map.59 = (f32[5,4,8,128]{3,2,1,0:T(8,128)S(1)}, f32[5,4,8,128]{3,2,1,0:T(8,128)S(1)}) custom-call(f32[5,4,8,128]{3,2,1,0:T(8,128)} %q_hbm.1, f32[9,4,8,128]{3,2,1,0:T(8,128)} %s_hbm.1, f32[4,8,128]{2,1,0:T(8,128)} %inv_hbm.1, s32[1,128]{1,0:T(1,128)} %bitcast.1), custom_call_target="tpu_custom_call" | custom-call | tf_op jit(solution)/shard_map/pallas_call | solution.py:722
  21.1 0.7 %shard_map.60 = (f32[5,4,8,128]{3,2,1,0:T(8,128)}, f32[5,4,8,128]{3,2,1,0:T(8,128)}) custom-call(f32[5,4,8,128]{3,2,1,0:T(8,128)S(1)} %get-tuple-element.4.state, f32[5,4,8,128]{3,2,1,0:T(8,128)S(1)} %get-tuple-element.5.rate), custom_call_target="tpu_custom_call" | custom-call | tf_op jit(solution)/shard_map/pallas_call | solution.py:752

commit v8 on v7

--- a/solution.py
+++ b/solution.py
@@ -417,6 +417,9 @@
     def fill(array, index):
         fields = [array[(m,) + index] for m in range(5)]
         metric = [array[(ROW + m,) + index] for m in range(3)]
+        put_terms(array, index, fields, metric)
+
+    def put_terms(array, index, fields, metric):
         fluxes, speed, velocity, pressure = cell_terms(fields, metric)
         for m in range(5):
             array[(FLUX + m,) + index] = fluxes[m]
@@ -575,6 +578,16 @@
         for out, flow, metric in raw_rows(2):
             halo = flow if flow is not None else 5 + metric
             ez[out, cell] = halo_ref[halo, plane]
+
+    def land(halo_ref, cell, plane):
+        cyclic = order_of(2)
+        fields = [halo_ref[m, plane] for m in (0, 1 + cyclic[0], 1 + cyclic[1], 1 + cyclic[2], 4)]
+        metric = [halo_ref[5 + member, plane] for member in cyclic]
+        for m in range(5):
+            ez[m, cell] = fields[m]
+        for m in range(3):
+            ez[ROW + m, cell] = metric[m]
+        put_terms(ez, (cell,), fields, metric)
 
     def take_z(halo_ref, base, low):
         for k in range(3):
@@ -661,14 +674,12 @@
             @pl.when(edge_low)
             def _():
                 far_arrive(ZL, stage)
-                take_plane(zl, 2 - stage, 3 - stage)
-                fill(ez, (2 - stage,))
+                land(zl, 2 - stage, 3 - stage)
 
             @pl.when(edge_high)
             def _():
                 far_arrive(ZH, stage)
-                take_plane(zh, 7 + stage, stage)
-                fill(ez, (7 + stage,))
+                land(zh, 7 + stage, stage)
 
             carry = face_z(jnp.where(edge_low, 2 - stage, 2 + stage), carry)
             finish(jnp.where(edge_low, 2 - stage, 1 + stage))

time: 21.9 us -> 21.9 us (level)
  no operation moved by 1% of the time
where the time goes in v8:
time: 21.9 us; the launch traced here: 21.8 us
  Pallas kernels  21.1 us (96%)
  between operations  0.64 us (3%)
    pallas_call x1, Pallas kernels, local(): pl.pallas_call(kernel, out_shape=(wide, wide), in_specs=[pl.BlockSpec(mem...  20.5 us
    pallas_call x1, Pallas kernels, local(): pl.pallas_call(deliver, out_shape=(jax.ShapeDtypeStruct(block, jnp.float3...  0.67 us

profile of v8, /device:TPU:6, one launch (start us, length us, event | category | flops | bytes accessed | tf_op | source)
XLA Modules:
  0.0 21.8 jit_solution(65479250761370917)
XLA Ops:
  0.6 20.5 %shard_map.59 = (f32[5,4,8,128]{3,2,1,0:T(8,128)S(1)}, f32[5,4,8,128]{3,2,1,0:T(8,128)S(1)}) custom-call(f32[5,4,8,128]{3,2,1,0:T(8,128)} %q_hbm.1, f32[9,4,8,128]{3,2,1,0:T(8,128)} %s_hbm.1, f32[4,8,128]{2,1,0:T(8,128)} %inv_hbm.1, s32[1,128]{1,0:T(1,128)} %bitcast.1), custom_call_target="tpu_custom_call" | custom-call | tf_op jit(solution)/shard_map/pallas_call | solution.py:733
  21.1 0.7 %shard_map.60 = (f32[5,4,8,128]{3,2,1,0:T(8,128)}, f32[5,4,8,128]{3,2,1,0:T(8,128)}) custom-call(f32[5,4,8,128]{3,2,1,0:T(8,128)S(1)} %get-tuple-element.4.state, f32[5,4,8,128]{3,2,1,0:T(8,128)S(1)} %get-tuple-element.5.rate), custom_call_target="tpu_custom_call" | custom-call | tf_op jit(solution)/shard_map/pallas_call | solution.py:763
